TPU v7x, 256 devices: a whole 4x4x8 slice. The times are simulated.
256 devices in a mesh: tm: 128 (over x, y_hi, z, core), chan: 2 (over y_lo).
Axes of the slice: x: 4, y: 4 (y_hi: 2, y_lo: 2; y = y_hi * 2 + y_lo), z: 8, core: 2. Of those that a mesh axis runs over, the one named last changes fastest.
Arguments:
- random_forcing: bfloat16 [49152, 4096], P('tm', 'chan'), may hold values from -6 to 6
- eigen_root_table: float32 [768, 4096], P(None, 'chan'), may hold values from 0.1 to 2
- lane_fading_speed: float32 [4096], P('chan'), may hold values from 4.0690104e-08 to 0.025, as said below
- sudden_shrink: float32 [49152], P('tm'), may hold values from 0.125 to 1, as said below
Outputs:
- sample: float32 [49152, 4096], P('tm', 'chan')
Inputs may be any that keep to these rules, and one draw needn't show every extreme that they name: `lane_fading_speed`: every channel's rate is positive. `sudden_shrink`: every entry lies in (0, 1], and the product of all entries is at most 0.52.
All inputs are finite; a program needn't handle non-finite values.
Results may differ from a plain program's by a relative error of at most 0.0003.
Values may be sent and summed in bfloat16 or wider, within the bound.
A program may use at most 192 MiB of HBM per device.

v0:
```python
import jax
import jax.numpy as jnp
from jax import lax
from jax.sharding import Mesh
from jax.sharding import PartitionSpec as P

TM = ("tm_0", "tm_1", "tm_2", "tm_3")


def from_behind(value, axis, steps):
    count = lax.axis_size(axis)
    pairs = [(source, (source + steps) % count) for source in range(count)]
    return lax.ppermute(value, axis, pairs)


def filled_with(array, identity):
    return jax.tree.map(
        lambda a, e: jnp.broadcast_to(jnp.asarray(e, a.dtype), a.shape), array, identity
    )


def collected_together(array, axis):
    leaves = jax.tree.leaves(array)
    order = sorted(range(len(leaves)), key=lambda k: -leaves[k].size)
    width = (1, *leaves[order[0]].shape)[-1]
    lines = [
        jnp.pad(leaves[k].reshape(-1), (0, -leaves[k].size % width)).reshape(-1, width)
        for k in order
    ]
    both, at, found = (lax.all_gather(jnp.concatenate(lines), axis), 0, {})
    for k, line in zip(order, lines):
        slab = both[:, at : at + len(line)].reshape(len(both), -1)
        found[k] = slab[:, : leaves[k].size].reshape(-1, *leaves[k].shape)
        at += len(line)
    numbers = iter(range(len(leaves)))
    return jax.tree.map(lambda _: found[next(numbers)], array)


def carried_in(array, axes, combine, identity):
    before = start = filled_with(array, identity)
    so_far = array
    for axis in reversed(axes):
        peers, position = (lax.axis_size(axis), lax.axis_index(axis))
        pieces = collected_together(so_far, axis)
        inside, so_far = (start, start)
        for k in range(peers):
            passed = k < position
            so_far = combine(so_far, jax.tree.map(lambda part: part[k], pieces))
            inside = jax.tree.map(lambda new, old: jnp.where(passed, new, old), so_far, inside)
        before = combine(inside, before)
    return before


def from_root(array, axes, root):
    array = jnp.where(lax.axis_index(axes) == root, array, jnp.zeros_like(array))
    for axis in axes:
        array = lax.psum(array, axis)
    return array


def combine(former, latter):
    return (former[0] + latter[0], jnp.exp(latter[0]) * former[1] + latter[1])


def tables(length):
    indices = jnp.arange(2 * length, dtype=jnp.int32)
    product = indices[:, None] * indices[None, :] % (2 * length)
    angles = product.astype(jnp.float32) * (jnp.pi / length)
    cosine = jnp.cos(angles)
    sine_table = jnp.sin(angles)
    forward = jnp.concatenate([cosine[:, :length], -sine_table[:, :length]], axis=0)
    inverse = jnp.concatenate([cosine, -sine_table], axis=1) / (2.0 * length)
    return (forward, inverse)


def spectra(segment, forward, spectrum, length):
    values = jnp.dot(
        forward,
        segment.astype(jnp.float32),
        precision=lax.Precision.HIGHEST,
        preferred_element_type=jnp.float32,
    )
    return jnp.concatenate(
        [spectrum * values[: 2 * length], spectrum * values[2 * length :]], axis=0
    )


def invert(scaled, inverse, first, count):
    return jnp.dot(
        inverse[first : first + count],
        scaled,
        precision=lax.Precision.HIGHEST,
        preferred_element_type=jnp.float32,
    )


def shards(random_forcing, eigen_root_table, lane_fading_speed, sudden_shrink):
    length = random_forcing.shape[0]
    width = random_forcing.shape[1]
    forward, inverse = tables(length)
    earlier_noise = from_behind(random_forcing, TM, 1)
    stacked = jnp.concatenate([random_forcing, earlier_noise], axis=1)
    doubled = jnp.concatenate([eigen_root_table, eigen_root_table], axis=1)
    scaled = spectra(stacked, forward, doubled, length)
    own_part = invert(scaled[:, :width], inverse, 0, length)
    earlier_part = invert(scaled[:, width:], inverse, length, length)
    noise_sequence = own_part + earlier_part
    tick_log_growth = jnp.log(sudden_shrink)[:, None] - lane_fading_speed[None, :]
    power_entries = (sudden_shrink * sudden_shrink)[:, None]
    weights = jnp.sqrt(
        1.0 - power_entries + power_entries * (-jnp.expm1(-2.0 * lane_fading_speed))[None, :]
    )
    rows = jnp.arange(length, dtype=jnp.int32)
    lower = (rows[:, None] >= rows[None, :]).astype(jnp.float32)
    logs = jnp.dot(
        lower, tick_log_growth, precision=lax.Precision.HIGHEST, preferred_element_type=jnp.float32
    )
    rescaled = jnp.exp(-logs) * (weights * noise_sequence)
    states = jnp.exp(logs) * jnp.dot(
        lower, rescaled, precision=lax.Precision.HIGHEST, preferred_element_type=jnp.float32
    )
    own_total = (logs[-1], states[-1])
    zeroes = jnp.zeros_like(own_total[0])
    preceding_input = carried_in(own_total, TM, combine, (zeroes, zeroes))
    through = combine(preceding_input, own_total)
    entire = (
        from_root(through[0], TM, lax.axis_size(TM) - 1),
        from_root(through[1], TM, lax.axis_size(TM) - 1),
    )
    opening = entire[1] / -jnp.expm1(entire[0])
    incoming = jnp.exp(preceding_input[0]) * opening + preceding_input[1]
    return states + jnp.exp(logs) * incoming[None, :]


def solution(mesh):
    torus = Mesh(
        mesh.devices.reshape(4, 2, 8, 2, mesh.shape["chan"]),
        ("tm_0", "tm_1", "tm_2", "tm_3", "chan"),
    )
    return jax.shard_map(
        shards,
        mesh=torus,
        in_specs=(P(TM, "chan"), P(None, "chan"), P("chan"), P(TM)),
        out_specs=P(TM, "chan"),
        check_vma=False,
    )
```

profile of v0, /device:TPU:1, one launch (start us, length us, event | category | flops | bytes accessed | tf_op | source)
XLA Modules:
  0.0 237.6 jit_solution(13609140888398446958)
XLA Ops:
  0.0 3.0 %collective-permute-start = (bf16[384,2048]{1,0:T(8,128)(2,1)}, bf16[384,2048]{1,0:T(8,128)(2,1)}, u32[]{:S(2)}, u32[]{:S(2)}) collective-permute-start(bf16[384,2048]{1,0:T(8,128)(2,1)} %param.4), channel_id=1, source_target_pairs={{0,2},{2,4},{4,6},{6,8},{8,10},{10,12},{12,14},{14,16},{16,18},{18... | collective-permute-start | bytes 4718600 | tf_op jit(solution)/shard_map/ppermute | solution.py:13
  3.0 10.5 %fusion.32 = (f32[768,768]{1,0:T(8,128)S(1)}, f32[768,768]{1,0:T(8,128)}) fusion(), kind=kLoop, calls=%fused_computation.39 | loop fusion | flops 5898240 | bytes 4718592 | tf_op jit(solution)/shard_map/cos | solution.py:69
  14.2 2.9 %fusion.18 = f32[384,2048]{1,0:T(8,128)S(1)} fusion(f32[2048]{0:T(1024)S(1)} %copy-done.11, f32[384]{0:T(512)S(1)} %get-tuple-element.39), kind=kOutput, calls=%fused_computation.25 | convolution fusion | flops 3624812544 | bytes 3155456 | tf_op jit(solution)/shard_map/dot_general | solution.py:115
  17.1 1.7 copy-done.3
  18.8 9.1 %fusion.31 = f32[768,768]{1,0:T(8,128)S(1)} fusion(), kind=kLoop, calls=%fused_computation.38 | loop fusion | flops 5308416 | bytes 2359296 | tf_op jit(solution)/shard_map/sin | solution.py:70
  28.0 3.4 %constant_dynamic-update-slice_fusion.1 = f32[768,4096]{1,0:T(8,128)S(1)} fusion(f32[768,2048]{1,0:T(8,128)} %param.5), kind=kLoop, calls=%fused_computation.112 | loop fusion | bytes 12582912
  33.4 0.9 copy-done.7
  34.3 2.8 %maximum_multiply_fusion = f32[768,1536]{1,0:T(8,128)} fusion(f32[768,768]{1,0:T(8,128)S(1)} %copy-done.7, f32[768,768]{1,0:T(8,128)S(1)} %get-tuple-element.40), kind=kLoop, calls=%fused_computation.9 | loop fusion | flops 2359296 | bytes 9437184 | tf_op jit(solution)/shard_map/div | solution.py:72
  37.1 2.5 %copy-done.1 = f32[768,4096]{1,0:T(8,128)} copy-done((f32[768,4096]{1,0:T(8,128)}, f32[768,4096]{1,0:T(8,128)S(1)}, u32[]{:S(2)}) %copy-start.1) | copy-done | bytes 12582936
  39.6 23.3 %fusion.5 = f32[1536,4096]{1,0:T(8,128)} fusion(bf16[384,2048]{1,0:T(8,128)(2,1)} %collective-permute-done, bf16[384,2048]{1,0:T(8,128)(2,1)S(1)} %copy-done.8, f32[768,384]{1,0:T(8,128)S(1)} %slice_negate_fusion, f32[768,384]{1,0:T(8,128)S(1)} %slice.241), kind=kOutput, calls=%fused_computation.11 | convolution fusion | flops 28997910528 | bytes 30670848 | tf_op jit(solution)/shard_map/dot_general | solution.py:77
  62.9 18.3 %slice_multiply_fusion = (f32[768,4096]{1,0:T(8,128)S(1)}, f32[768,4096]{1,0:T(8,128)}) fusion(f32[768,4096]{1,0:T(8,128)} %copy-done.1, f32[1536,4096]{1,0:T(8,128)} %fusion.5), kind=kLoop, calls=%fused_computation.7 | loop fusion | flops 6291456 | bytes 62914560 | tf_op jit(solution)/shard_map/mul | solution.py:84
  81.3 19.2 %fusion.3 = f32[384,2048]{1,0:T(8,128)} fusion(f32[768,4096]{1,0:T(8,128)S(1)} %get-tuple-element.28, f32[768,4096]{1,0:T(8,128)} %get-tuple-element.29, f32[768,1536]{1,0:T(8,128)} %maximum_multiply_fusion), kind=kOutput, calls=%fused_computation.5 | convolution fusion | flops 14498660352 | bytes 30670848 | tf_op jit(solution)/shard_map/dot_general | solution.py:89
  100.5 17.2 %fusion.1 = f32[384,2048]{1,0:T(8,128)} fusion(f32[768,4096]{1,0:T(8,128)S(1)} %copy-done, f32[768,4096]{1,0:T(8,128)S(1)} %get-tuple-element.28, f32[768,1536]{1,0:T(8,128)S(1)} %copy-done.2), kind=kOutput, calls=%fused_computation.3 | convolution fusion | flops 14498660352 | bytes 30670848 | tf_op jit(solution)/shard_map/dot_general | solution.py:89
  117.7 6.5 %exponential_multiply_fusion = f32[384,2048]{1,0:T(8,128)S(1)} fusion(f32[384,2048]{1,0:T(8,128)S(1)} %copy-done.4, f32[384,2048]{1,0:T(8,128)} %fusion.1, f32[384,2048]{1,0:T(8,128)} %fusion.3, f32[2048]{0:T(1024)S(1)} %exponential-minus-one_negate_fusion, f32[384]{0:T(512)S(1)} %copy-done.10, f32[384]{0:T(512)S(1)} %copy-done.9), kind=kOutput, calls=%fused_computation.27 | convolution fusion | flops 3629531136 | bytes 12594176 | tf_op jit(solution)/shard_map/dot_general | solution.py:119
  124.2 1.6 copy-done.6
  125.9 1.8 all-gather.4
  127.8 21.2 %all-gather.5 = f32[8,2,2048]{2,1,0:T(2,128)S(1)} all-gather(f32[1,2,2048]{2,1,0:T(2,128)S(1)} %maximum_bitcast_fusion.1), channel_id=3, replica_groups=mesh['tm_0'=4,'tm_1'=2,'tm_2'=8,'tm_3'=2,'chan'=2] {'tm_2'}, dimensions={0}, use_global_device_ids=true | all-gather | bytes 147456 | tf_op jit(solution)/shard_map/all_gather | solution.py:30
  149.3 4.8 %all-gather.6 = f32[2,2,2048]{2,1,0:T(2,128)S(1)} all-gather(f32[1,2,2048]{2,1,0:T(2,128)S(1)} %maximum_bitcast_fusion.2), channel_id=4, replica_groups=mesh['tm_0'=4,'tm_1'=2,'tm_2'=8,'tm_3'=2,'chan'=2] {'tm_1'}, dimensions={0}, use_global_device_ids=true | all-gather | bytes 49152 | tf_op jit(solution)/shard_map/all_gather | solution.py:30
  154.1 9.3 %all-gather.7 = f32[4,2,2048]{2,1,0:T(2,128)S(1)} all-gather(f32[1,2,2048]{2,1,0:T(2,128)S(1)} %maximum_bitcast_fusion.3), channel_id=5, replica_groups=mesh['tm_0'=4,'tm_1'=2,'tm_2'=8,'tm_3'=2,'chan'=2] {'tm_0'}, dimensions={0}, use_global_device_ids=true | all-gather | bytes 81920 | tf_op jit(solution)/shard_map/all_gather | solution.py:30
  163.7 12.8 %all-reduce.1 = (f32[2048]{0:T(1024)S(1)}, f32[2048]{0:T(1024)S(1)}) all-reduce(f32[2048]{0:T(1024)S(1)} %get-tuple-element.16, f32[2048]{0:T(1024)S(1)} %get-tuple-element.36), channel_id=1, replica_groups=mesh['tm_0'=4,'tm_1'=2,'tm_2'=8,'tm_3'=2,'chan'=2] {'tm_0'}, use_global_device_ids=true, to_apply=%region_0.1 | all-reduce | flops 4096 | bytes 32768 | tf_op jit(solution)/shard_map/psum | solution.py:57
  176.5 9.2 %all-reduce.3 = (f32[2048]{0:T(1024)S(1)}, f32[2048]{0:T(1024)S(1)}) all-reduce(f32[2048]{0:T(1024)S(1)} %get-tuple-element.7, f32[2048]{0:T(1024)S(1)} %get-tuple-element.8), channel_id=1, replica_groups=mesh['tm_0'=4,'tm_1'=2,'tm_2'=8,'tm_3'=2,'chan'=2] {'tm_1'}, use_global_device_ids=true, to_apply=%region_1.2 | all-reduce | flops 4096 | bytes 32768 | tf_op jit(solution)/shard_map/psum | solution.py:57
  185.7 20.9 %all-reduce = (f32[2048]{0:T(1024)S(1)}, f32[2048]{0:T(1024)S(1)}) all-reduce(f32[2048]{0:T(1024)S(1)} %get-tuple-element.11, f32[2048]{0:T(1024)S(1)} %get-tuple-element.12), channel_id=1, replica_groups=mesh['tm_0'=4,'tm_1'=2,'tm_2'=8,'tm_3'=2,'chan'=2] {'tm_2'}, use_global_device_ids=true, to_apply=%region_2.3 | all-reduce | flops 4096 | bytes 32768 | tf_op jit(solution)/shard_map/psum | solution.py:57
  206.7 26.6 %all-reduce.2 = (f32[2048]{0:T(1024)S(1)}, f32[2048]{0:T(1024)S(1)}) all-reduce(f32[2048]{0:T(1024)S(1)} %get-tuple-element.5, f32[2048]{0:T(1024)S(1)} %get-tuple-element.6), channel_id=1, replica_groups=mesh['tm_0'=4,'tm_1'=2,'tm_2'=8,'tm_3'=2,'chan'=2] {'tm_3'}, use_global_device_ids=true, to_apply=%region_3.4 | all-reduce | flops 4096 | bytes 32768 | tf_op jit(solution)/shard_map/psum | solution.py:57
  233.3 4.3 %multiply_add_fusion = f32[384,2048]{1,0:T(8,128)} fusion(f32[384,2048]{1,0:T(8,128)} %copy-done.6, f32[384,2048]{1,0:T(8,128)S(1)} %copy-done.5, f32[2048]{0:T(1024)S(1)} %multiply_add_fusion.1), kind=kLoop, calls=%fused_computation.15 | loop fusion | flops 1572864 | bytes 9445376 | tf_op jit(solution)/shard_map/add | solution.py:132
  (50 shorter events, 3.5 us)
Async XLA Ops:
  0.0 13.6 %copy-start.12 = (f32[384]{0:T(512)S(1)}, f32[384]{0:T(512)}, u32[]{:S(2)}) copy-start(f32[384]{0:T(512)} %param.7) | copy-start | bytes 4612
  0.0 14.2 %copy-start.11 = (f32[2048]{0:T(1024)S(1)}, f32[2048]{0:T(1024)}, u32[]{:S(2)}) copy-start(f32[2048]{0:T(1024)} %param.6) | copy-start | bytes 24580
  0.0 37.1 %collective-permute-start = (bf16[384,2048]{1,0:T(8,128)(2,1)}, bf16[384,2048]{1,0:T(8,128)(2,1)}, u32[]{:S(2)}, u32[]{:S(2)}) collective-permute-start(bf16[384,2048]{1,0:T(8,128)(2,1)} %param.4), channel_id=1, source_target_pairs={{0,2},{2,4},{4,6},{6,8},{8,10},{10,12},{12,14},{14,16},{16,18},{18... | collective-permute-start | bytes 4718600 | tf_op jit(solution)/shard_map/ppermute | solution.py:13
  17.1 1.7 copy-start.3
  27.9 4.0 %slice-start = ((s8[6291456]{0:T(1024)(128)(4,1)}), s8[4194304]{0:T(1024)(128)(4,1)S(1)}, s32[]{:S(2)}) async-start(s8[6291456]{0:T(1024)(128)(4,1)} %bitcast.30), calls=%async_computation | async-start | bytes 8388608
  28.0 4.6 %slice-start.1 = ((s8[6291456]{0:T(1024)(128)(4,1)}), s8[2097152]{0:T(1024)(128)(4,1)S(1)}, s32[]{:S(2)}) async-start(s8[6291456]{0:T(1024)(128)(4,1)} %bitcast.30), calls=%async_computation.1 | async-start | bytes 4194304
  32.6 1.7 copy-start.7
  33.4 6.2 %copy-start.1 = (f32[768,4096]{1,0:T(8,128)}, f32[768,4096]{1,0:T(8,128)S(1)}, u32[]{:S(2)}) copy-start(f32[768,4096]{1,0:T(8,128)S(1)} %constant_dynamic-update-slice_fusion) | copy-start | bytes 37748740
  34.3 5.3 %copy-start.8 = (bf16[384,2048]{1,0:T(8,128)(2,1)S(1)}, bf16[384,2048]{1,0:T(8,128)(2,1)}, u32[]{:S(2)}) copy-start(bf16[384,2048]{1,0:T(8,128)(2,1)} %param.4) | copy-start | bytes 4718596
  81.3 19.2 %copy-start = (f32[768,4096]{1,0:T(8,128)S(1)}, f32[768,4096]{1,0:T(8,128)}, u32[]{:S(2)}) copy-start(f32[768,4096]{1,0:T(8,128)} %get-tuple-element.29) | copy-start | bytes 37748740
  81.3 19.2 %copy-start.2 = (f32[768,1536]{1,0:T(8,128)S(1)}, f32[768,1536]{1,0:T(8,128)}, u32[]{:S(2)}) copy-start(f32[768,1536]{1,0:T(8,128)} %maximum_multiply_fusion) | copy-start | bytes 14155780
  100.5 17.2 %copy-start.4 = (f32[384,2048]{1,0:T(8,128)S(1)}, f32[384,2048]{1,0:T(8,128)}, u32[]{:S(2)}) copy-start(f32[384,2048]{1,0:T(8,128)} %copy-done.3) | copy-start | bytes 9437188
  100.5 17.2 %copy-start.9 = (f32[384]{0:T(512)S(1)}, f32[384]{0:T(512)}, u32[]{:S(2)}) copy-start(f32[384]{0:T(512)} %get-tuple-element.37) | copy-start | bytes 4612
  100.5 17.2 %copy-start.10 = (f32[384]{0:T(512)S(1)}, f32[384]{0:T(512)}, u32[]{:S(2)}) copy-start(f32[384]{0:T(512)} %get-tuple-element.38) | copy-start | bytes 4612
  117.7 115.6 %copy-start.5 = (f32[384,2048]{1,0:T(8,128)S(1)}, f32[384,2048]{1,0:T(8,128)}, u32[]{:S(2)}) copy-start(f32[384,2048]{1,0:T(8,128)} %copy-done.3) | copy-start | bytes 9437188
  124.2 1.7 copy-start.6
where the time goes:
time: 238 us
  blocking collectives  107 us (45%)
  matrix products  69.1 us (29%)
  other arithmetic  46.3 us (19%)
  local copies, waits for them, and re-layouts  12.2 us (5%)
  starting transfers between devices  3.02 us (1%)
    psum x4, blocking collectives, from_root(): array = lax.psum(array, axis)  69.6 us
    all_gather x4, blocking collectives, collected_together(): both, at, found = (lax.all_gather(jnp.concatenate(lines), axis), 0, {})  37.1 us
    dot_general x2, matrix products, invert(): jnp.dot(inverse[first:first + count], scaled, precision=lax.Precision.HIG...  36.4 us
    dot_general x1, matrix products, spectra(): jnp.dot(forward, segment.astype(jnp.float32), precision=lax.Precision.HIG...  23.3 us
    mul x1, other arithmetic, spectra(): spectrum * values[2 * length:]  18.3 us
    unnamed x31, local copies, waits for them, and re-layouts  11.3 us
    cos x1, other arithmetic, tables(): cosine = jnp.cos(angles)  10.5 us
    sin x1, other arithmetic, tables(): sine_table = jnp.sin(angles)  9.06 us
  transfers between devices with their start and end apart: 1, of which 0 were waited for; matrix products, arithmetic and copies ran while one was open for 13% of the time, Pallas kernels for 0%

commit v1 on v0

v1 whole, which is shorter than its diff:
```python
import functools

import jax
import jax.numpy as jnp
import ml_dtypes
import numpy as np
from jax import lax
from jax.experimental import pallas as pl
from jax.experimental.pallas import tpu as pltpu
from jax.sharding import PartitionSpec as P

MESH = pl.DeviceIdType.MESH
F32 = jnp.float32
BF16 = jnp.bfloat16
MEMBERS = 16


def split(table):
    high = table.astype(ml_dtypes.bfloat16)
    low = (table - high.astype(np.float64)).astype(ml_dtypes.bfloat16)
    return high, low


@functools.lru_cache
def tables(length):
    half = length // 2
    t = np.arange(length)
    even = 2 * np.arange(half)
    odd = even + 1

    def basis(f, function):
        return function(2.0 * np.pi * (np.outer(f, t) % (2 * length)) / (2 * length))

    even_sine = basis(even, np.sin)
    even_sine[0] = np.cos(np.pi * t)
    rows = np.concatenate([basis(even, np.cos), even_sine, basis(odd, np.cos), basis(odd, np.sin)])
    forward = np.concatenate(split(rows), axis=1)
    runs = length // 8
    order = (np.arange(8)[None, :] * runs + np.arange(runs)[:, None]).reshape(-1)
    high, low = split(rows.T[order])
    parts = []
    for k in range(2):
        at = slice(k * length, (k + 1) * length)
        parts += [high[:, at], high[:, at], low[:, at]]
    return forward, np.concatenate(parts, axis=1)


def flipped(tile):
    at = 7 - lax.broadcasted_iota(jnp.int32, tile.shape, 0)
    return jnp.take_along_axis(tile, at, axis=0)


def fold(e_ref, es_ref, lane, length):
    half = length // 2
    scale = 1.0 / (2 * length)
    row = lax.broadcasted_iota(jnp.int32, (8, 128), 0)
    for b in range(half // 8):
        value = e_ref[lane, pl.ds(16 * b, 8, stride=2), :]
        if b:
            mirror = flipped(e_ref[lane, pl.ds(2 * length - 14 - 16 * b, 8, stride=2), :])
        else:
            mirror = flipped(e_ref[lane, pl.ds(2 * length - 16, 8, stride=2), :])
            mirror = jnp.where(row == 0, 0.0, pltpu.roll(mirror, 1, 0))
        total = (value + mirror) * scale
        es_ref[lane, 8 * b : 8 * b + 8, :] = total
        if b == 0:
            middle = jnp.broadcast_to(e_ref[lane, length : length + 1, :], (8, 128)) * scale
            total = jnp.where(row == 0, middle, total)
        es_ref[lane, half + 8 * b : half + 8 * b + 8, :] = total
        value = e_ref[lane, pl.ds(16 * b + 1, 8, stride=2), :]
        mirror = flipped(e_ref[lane, pl.ds(2 * length - 15 - 16 * b, 8, stride=2), :])
        es_ref[lane, 2 * half + 8 * b : 2 * half + 8 * b + 8, :] = (value + mirror) * scale


def over_runs(state, decay):
    row = lax.broadcasted_iota(jnp.int32, state.shape, 0)
    for step in (1, 2, 4):
        reach = row >= step
        state = jnp.where(reach, decay * pltpu.roll(state, step, 0) + state, state)
        decay = jnp.where(reach, decay * pltpu.roll(decay, step, 0), decay)
    return state, decay


def weight(burst, spread):
    power = burst * burst
    return jnp.sqrt((1.0 - power) + power * spread)


def fields(
    length, sections, v_hbm, e_hbm, forward_hbm, inverse_hbm, rows_ref, rate_ref, burst_ref, logs_ref,
    x_ref, carry_ref, reach_ref, grown_ref, incoming_ref,
    v_ref, e_ref, forward_ref, inverse_ref, es_ref, earlier_ref, twice_ref, value_ref, scaled_ref, p_ref, q_ref, lead_ref,
    own_ref, next_ref, next_burst_ref, ends_ref, a_ref, c_ref, c_in_ref, half_ref, pair_ref, chips_ref, groups_ref,
    member_logs_ref, group_logs_ref, group_log_ref, chip_out_ref, group_out_ref, give_ref, take_ref,
    v_sem, e_sem, t_sem, noise_send, noise_recv, burst_sem, c_sem, pair_sem, give_sem,
    logs_send, logs_recv, chips_send, chips_recv, groups_send, groups_recv, glogs_send, glogs_recv,
):
    width = v_hbm.shape[1]
    chunk = 256
    chunks = width // chunk
    lanes = width // 128
    half = length // 2
    runs = length // 8
    groups = sections // MEMBERS
    chips = MEMBERS // 2
    me = lax.axis_index("tm")
    group, member = me // MEMBERS, me % MEMBERS
    chip, core = member // 2, member % 2
    after, before = (me + 1) % sections, (me + sections - 1) % sections
    partner = group * MEMBERS + chip * 2 + (1 - core)

    def remote(source, target, send, recv, device):
        return pltpu.make_async_remote_copy(
            src_ref=source, dst_ref=target, send_sem=send, recv_sem=recv, device_id={"tm": device}, device_id_type=MESH
        )

    def columns(i):
        return pl.ds(pl.multiple_of(i * chunk, chunk), chunk)

    members = [group * MEMBERS + (member + k) % MEMBERS for k in range(1, MEMBERS)]
    chip_peers = [group * MEMBERS + ((chip + k) % chips) * 2 + core for k in range(1, chips)]
    group_peers = [((group + k) % groups) * MEMBERS + member for k in range(1, groups)]

    barrier = pltpu.get_barrier_semaphore()
    for device in [after, before] + members + group_peers:
        pl.semaphore_signal(barrier, inc=1, device_id={"tm": device}, device_id_type=MESH)

    local = [
        pltpu.make_async_copy(v_hbm, v_ref.at[pl.ds(0, length)], v_sem.at[0]),
        pltpu.make_async_copy(v_hbm, v_ref.at[pl.ds(length, length)], v_sem.at[1]),
        pltpu.make_async_copy(forward_hbm, forward_ref, t_sem.at[0]),
        pltpu.make_async_copy(inverse_hbm, inverse_ref, t_sem.at[1]),
    ]

    def table(lane):
        return pltpu.make_async_copy(e_hbm.at[:, pl.ds(pl.multiple_of(lane * 128, 128), 128)], e_ref.at[lane], e_sem.at[lane])

    for lane in range(lanes):
        table(lane).start()
    for copy in local:
        copy.start()

    product = jnp.ones((8, 128), F32)
    for j in range(runs):
        column = jnp.broadcast_to(burst_ref[:, j : j + 1], (8, 128))
        own_ref[8 * j : 8 * j + 8, :] = column
        product = product * column
        grown_ref[8 * j : 8 * j + 8, :] = product
    ends_ref[0] = product

    pl.semaphore_wait(barrier, 2 + (MEMBERS - 1) + (groups - 1))

    burst_copy = remote(burst_ref, next_burst_ref, burst_sem.at[0], burst_sem.at[1], before)
    burst_copy.start()
    logs_copies = [
        remote(logs_ref, member_logs_ref.at[member], logs_send.at[k], logs_recv.at[k], device)
        for k, device in enumerate(members)
    ]
    for copy in logs_copies:
        copy.start()

    def noise(i):
        return remote(v_hbm.at[:, columns(i)], earlier_ref.at[:, columns(i)], noise_send.at[i], noise_recv.at[i], after)

    noise(0).start()
    noise(1).start()

    def fold_step(lane, carry):
        table(lane).wait()
        fold(e_ref, es_ref, lane, length)
        return carry

    lax.fori_loop(0, lanes, fold_step, 0)

    for copy in local:
        copy.wait()
    burst_copy.wait()
    product = jnp.ones((8, 128), F32)
    for j in range(runs):
        column = jnp.broadcast_to(next_burst_ref[:, j : j + 1], (8, 128))
        next_ref[8 * j : 8 * j + 8, :] = column
        product = product * column
    ends_ref[1] = product

    def transform(i, data, sign):
        value_ref[...] = jnp.dot(forward_ref[...], data, preferred_element_type=F32)
        for part in range(4):
            at = (0, half, 2 * half, 2 * half)[part]
            base = 3 * length * (part // 2) + half * (part % 2)
            for side in range(2):
                cut = slice(128 * side, 128 * side + 128)
                scaled = value_ref[half * part : half * part + half, cut] * es_ref[2 * i + side, at : at + half, :]
                if part >= 2 and sign < 0:
                    scaled = -scaled
                high = scaled.astype(BF16)
                low = (scaled - high.astype(F32)).astype(BF16)
                scaled_ref[base : base + half, cut] = high
                scaled_ref[base + length : base + length + half, cut] = low
                scaled_ref[base + 2 * length : base + 2 * length + half, cut] = high

    def row_of(index, lane_columns):
        return jnp.broadcast_to(rows_ref[index : index + 1, lane_columns], (8, 128))

    def early(i, carry):
        transform(i, v_ref[:, columns(i)], 1)
        cut = 3 * length
        p_ref[...] = jnp.dot(inverse_ref[:, :cut], scaled_ref[:cut, :], preferred_element_type=F32)
        q_ref[...] = jnp.dot(inverse_ref[:, cut:], scaled_ref[cut:, :], preferred_element_type=F32)
        for side in range(2):
            lane = 2 * i + side
            cols = pl.ds(pl.multiple_of(lane * 128, 128), 128)
            keep, keep_run, spread = row_of(0, cols), row_of(1, cols), row_of(2, cols)
            here = jnp.zeros((8, 128), F32)
            there = jnp.zeros((8, 128), F32)
            for j in range(runs):
                at = slice(8 * j, 8 * j + 8)
                p = p_ref[at, 128 * side : 128 * side + 128]
                q = q_ref[at, 128 * side : 128 * side + 128]
                lead = p + q
                lead_ref[lane, at, :] = lead
                burst = own_ref[at, :]
                here = (burst * keep) * here + weight(burst, spread) * lead
                burst = next_ref[at, :]
                there = (burst * keep) * there + weight(burst, spread) * (p - q)
            here, _ = over_runs(here, ends_ref[0] * keep_run)
            there, _ = over_runs(there, ends_ref[1] * keep_run)
            a_ref[pl.ds(lane, 1), :] = here[7:8, :]
            c_ref[pl.ds(lane, 1), :] = there[7:8, :]

        @pl.when((i % 2 == 1) & (i < chunks - 1))
        def _():
            noise(2 + i // 2).start()

        return carry

    lax.fori_loop(0, chunks, early, 0)

    c_copy = remote(c_ref, c_in_ref, c_sem.at[0], c_sem.at[1], after)
    c_copy.start()
    sent_early = 2 + (chunks - 1) // 2

    for copy in logs_copies:
        copy.wait()
    member_logs_ref[pl.ds(member, 1)] = logs_ref[...].reshape(1, 1, 128)
    logs_of = [jnp.broadcast_to(member_logs_ref[k], (8, 128)) for k in range(MEMBERS)]
    whole = sum(logs_of[1:], logs_of[0])
    group_log_ref[...] = whole[0:1, :]
    group_logs_ref[pl.ds(group, 1)] = whole[0:1, :].reshape(1, 1, 128)
    glogs_copies = [
        remote(group_log_ref, group_logs_ref.at[group], glogs_send.at[k], glogs_recv.at[k], device)
        for k, device in enumerate(group_peers)
    ]
    for copy in glogs_copies:
        copy.start()

    own_half = pl.ds(pl.multiple_of(core * 8, 8), 8)
    other_half = pl.ds(pl.multiple_of((1 - core) * 8, 8), 8)
    pair_copy = remote(half_ref.at[0], pair_ref, pair_sem.at[0], pair_sem.at[1], partner)
    chip_copies = [
        remote(chip_out_ref, chips_ref.at[chip], chips_send.at[k], chips_recv.at[k], device)
        for k, device in enumerate(chip_peers)
    ]
    group_copies = [
        remote(group_out_ref, groups_ref.at[group], groups_send.at[k], groups_recv.at[k], device)
        for k, device in enumerate(group_peers)
    ]
    give_copy = remote(give_ref, take_ref, give_sem.at[0], give_sem.at[1], partner)

    def log_of(index):
        return jnp.broadcast_to(member_logs_ref[index], (8, 128))

    def pair_states():
        mine, theirs = half_ref[1], pair_ref[...]
        first = jnp.where(core == 0, mine, theirs)
        second = jnp.where(core == 0, theirs, mine)
        return first, second

    def exchange_pair():
        c_copy.wait()
        half_ref[0] = a_ref[other_half, :] + c_in_ref[other_half, :]
        half_ref[1] = a_ref[own_half, :] + c_in_ref[own_half, :]
        pair_copy.start()

    def exchange_chips():
        pair_copy.wait()
        first, second = pair_states()
        rate = rate_ref[own_half, :]
        total = jnp.exp(log_of(2 * chip + 1)[0:8] - length * rate) * first + second
        chip_out_ref[...] = total
        chips_ref[pl.ds(chip, 1)] = total.reshape(1, 8, 128)
        for copy in chip_copies:
            copy.start()

    def exchange_groups():
        for copy in chip_copies:
            copy.wait()
        rate = rate_ref[own_half, :]
        state = jnp.zeros((8, 128), F32)
        log = jnp.zeros((8, 128), F32)
        before_state, before_log = state, log
        for k in range(chips):
            here = chip == k
            before_state = jnp.where(here, state, before_state)
            before_log = jnp.where(here, log, before_log)
            step = (log_of(2 * k) + log_of(2 * k + 1)) - (2 * length) * rate
            state = jnp.exp(step) * state + chips_ref[k]
            log = log + step
        half_ref[2] = before_state
        half_ref[3] = before_log
        group_out_ref[...] = state
        groups_ref[pl.ds(group, 1)] = state.reshape(1, 8, 128)
        for copy in group_copies:
            copy.start()

    def exchange_back():
        for copy in group_copies:
            copy.wait()
        for copy in glogs_copies:
            copy.wait()
        rate = rate_ref[own_half, :]
        state = jnp.zeros((8, 128), F32)
        log = jnp.zeros((8, 128), F32)
        for k in range(groups):
            at = (group + k) % groups
            step = jnp.broadcast_to(group_logs_ref[at], (8, 128)) - (MEMBERS * length) * rate
            state = jnp.exp(step) * state + groups_ref[at]
            log = log + step
        opening = state / (1.0 - jnp.exp(log))
        first_in = jnp.exp(half_ref[3]) * opening + half_ref[2]
        first, _ = pair_states()
        second_in = jnp.exp(log_of(2 * chip) - length * rate) * first_in + first
        incoming_ref[own_half, :] = jnp.where(core == 0, first_in, second_in)
        give_ref[...] = jnp.where(core == 0, second_in, first_in)
        give_copy.start()

    def late(i, carry):
        @pl.when(i + sent_early < chunks)
        def _():
            noise(i + sent_early).start()

        noise(i).wait_recv()
        block = earlier_ref[:, columns(i)]
        twice_ref[0:length, :] = block
        twice_ref[length : 2 * length, :] = block
        transform(i, twice_ref[...], -1)
        p_ref[...] = jnp.dot(inverse_ref[...], scaled_ref[...], preferred_element_type=F32)
        for side in range(2):
            lane = 2 * i + side
            cols = pl.ds(pl.multiple_of(lane * 128, 128), 128)
            keep, keep_run, spread = row_of(0, cols), row_of(1, cols), row_of(2, cols)
            state = jnp.zeros((8, 128), F32)
            for j in range(runs):
                at = slice(8 * j, 8 * j + 8)
                burst = own_ref[at, :]
                series = lead_ref[lane, at, :] + p_ref[at, 128 * side : 128 * side + 128]
                state = (burst * keep) * state + weight(burst, spread) * series
                x_ref[lane, at, :] = state
            state, decay = over_runs(state, ends_ref[0] * keep_run)
            row = lax.broadcasted_iota(jnp.int32, (8, 128), 0)
            carry_ref[lane] = jnp.where(row == 0, 0.0, pltpu.roll(state, 1, 0))
            reach_ref[lane] = jnp.where(row == 0, 1.0, pltpu.roll(decay, 1, 0))
        for at, step in ((1, exchange_pair), (2, exchange_chips), (4, exchange_groups), (6, exchange_back)):
            pl.when(i == at)(step)
        return carry

    lax.fori_loop(0, chunks, late, 0)
    give_copy.wait()
    incoming_ref[other_half, :] = take_ref[...]

    def drain(i, carry):
        noise(i).wait_send()
        return carry

    lax.fori_loop(0, chunks, drain, 0)


def close(length, x_ref, carry_ref, reach_ref, grown_ref, incoming_ref, rows_ref, out_hbm, stage_ref, sem):
    lanes = x_ref.shape[0]
    runs = length // 8

    def out(lane):
        return pltpu.make_async_copy(
            stage_ref.at[lane], out_hbm.at[:, pl.ds(pl.multiple_of(lane * 128, 128), 128)], sem.at[lane]
        )

    def step(lane, carry):
        cols = pl.ds(pl.multiple_of(lane * 128, 128), 128)
        keep = jnp.broadcast_to(rows_ref[0:1, cols], (8, 128))
        incoming = jnp.broadcast_to(incoming_ref[pl.ds(lane, 1), :], (8, 128))
        state = (carry_ref[lane] + reach_ref[lane] * incoming) * keep
        for j in range(runs):
            at = slice(8 * j, 8 * j + 8)
            stage_ref[lane, pl.ds(j, 8, stride=runs), :] = x_ref[lane, at, :] + grown_ref[at, :] * state
            state = state * keep
        out(lane).start()
        return carry

    lax.fori_loop(0, lanes, step, 0)

    def drain(lane, carry):
        out(lane).wait()
        return carry

    lax.fori_loop(0, lanes, drain, 0)


def shards(sections, random_forcing, eigen_root_table, lane_fading_speed, sudden_shrink):
    length, width = random_forcing.shape
    lanes, runs, half = width // 128, length // 8, length // 2
    chunk = 256
    chunks = width // chunk
    groups, chips = sections // MEMBERS, MEMBERS // 2
    forward, inverse = tables(length)
    rate = lane_fading_speed
    rows = jnp.stack([jnp.exp(-rate), jnp.exp(-runs * rate), -jnp.expm1(-2.0 * rate)])
    rows = jnp.pad(rows, ((0, 5), (0, 0)))
    burst = jnp.pad(sudden_shrink.reshape(8, runs), ((0, 0), (0, 128 - runs)))
    logs = jnp.broadcast_to(jnp.sum(jnp.log(sudden_shrink)), (1, 128))
    anywhere = pl.BlockSpec(memory_space=pl.ANY)
    vmem = pl.BlockSpec(memory_space=pltpu.VMEM)
    dma = pltpu.SemaphoreType.DMA
    tile = pltpu.VMEM((8, 128), F32)
    results = pl.pallas_call(
        functools.partial(fields, length, sections),
        name="fields",
        out_shape=[
            jax.ShapeDtypeStruct((lanes, length, 128), F32),
            jax.ShapeDtypeStruct((lanes, 8, 128), F32),
            jax.ShapeDtypeStruct((lanes, 8, 128), F32),
            jax.ShapeDtypeStruct((length, 128), F32),
            jax.ShapeDtypeStruct((lanes, 128), F32),
        ],
        in_specs=[anywhere] * 4 + [vmem] * 4,
        out_specs=[vmem] * 5,
        scratch_shapes=[
            pltpu.VMEM((2 * length, width), BF16),
            pltpu.VMEM((lanes, 2 * length, 128), F32),
            pltpu.VMEM((2 * length, 2 * length), BF16),
            pltpu.VMEM((length, 6 * length), BF16),
            pltpu.VMEM((lanes, 3 * half, 128), F32),
            pltpu.VMEM((length, width), BF16),
            pltpu.VMEM((2 * length, chunk), BF16),
            pltpu.VMEM((2 * length, chunk), F32),
            pltpu.VMEM((6 * length, chunk), BF16),
            pltpu.VMEM((length, chunk), F32),
            pltpu.VMEM((length, chunk), F32),
            pltpu.VMEM((lanes, length, 128), F32),
            pltpu.VMEM((length, 128), F32),
            pltpu.VMEM((length, 128), F32),
            tile,
            pltpu.VMEM((2, 8, 128), F32),
            pltpu.VMEM((lanes, 128), F32),
            pltpu.VMEM((lanes, 128), F32),
            pltpu.VMEM((lanes, 128), F32),
            pltpu.VMEM((4, 8, 128), F32),
            tile,
            pltpu.VMEM((chips, 8, 128), F32),
            pltpu.VMEM((groups, 8, 128), F32),
            pltpu.VMEM((MEMBERS, 1, 128), F32),
            pltpu.VMEM((groups, 1, 128), F32),
            pltpu.VMEM((1, 128), F32),
            tile,
            tile,
            tile,
            tile,
            dma((2,)),
            dma((lanes,)),
            dma((2,)),
            dma((chunks,)),
            dma((chunks,)),
            dma((2,)),
            dma((2,)),
            dma((2,)),
            dma((2,)),
            dma((MEMBERS - 1,)),
            dma((MEMBERS - 1,)),
            dma((chips - 1,)),
            dma((chips - 1,)),
            dma((groups - 1,)),
            dma((groups - 1,)),
            dma((groups - 1,)),
            dma((groups - 1,)),
        ],
        compiler_params=pltpu.CompilerParams(
            collective_id=0, has_side_effects=True, vmem_limit_bytes=48 * 2**20
        ),
    )(random_forcing, eigen_root_table, jnp.asarray(forward), jnp.asarray(inverse), rows, rate.reshape(lanes, 128), burst, logs)
    return pl.pallas_call(
        functools.partial(close, length),
        name="close",
        out_shape=jax.ShapeDtypeStruct((length, width), F32),
        in_specs=[vmem] * 6,
        out_specs=anywhere,
        scratch_shapes=[pltpu.VMEM((lanes, length, 128), F32), dma((lanes,))],
    )(*results, rows)


def solution(mesh):
    return jax.shard_map(
        functools.partial(shards, mesh.shape["tm"]),
        mesh=mesh,
        in_specs=(P("tm", "chan"), P(None, "chan"), P("chan"), P("tm")),
        out_specs=P("tm", "chan"),
        check_vma=False,
    )
```

time: 238 us -> 64.2 us (0.27)
  blocking collectives: 107 us -> 0 us
  matrix products: 69.1 us -> 0 us
  Pallas kernels: 0 us -> 53 us
  other arithmetic: 46.3 us -> 2.04 us
  local copies, waits for them, and re-layouts: 12.2 us -> 8.79 us
  starting transfers between devices: 3.02 us -> 0 us
    psum x4 -> x0, blocking collectives: 69.6 us -> none  [from_root(): array = lax.psum(array, axis)]
    dot_general x5 -> x0, matrix products: 69.1 us -> none  [the longest x2 36.4 us: invert(): jnp.dot(inverse[first:first + count], scaled, precision=lax.Precision.HIG...]
    pallas_call x0 -> x2, Pallas kernels: none -> 53 us  [the longest x1 49 us: shards(): pl.pallas_call(functools.partial(fields, length, sections), name='fields'...]
    all_gather x4 -> x0, blocking collectives: 37.1 us -> none  [collected_together(): both, at, found = (lax.all_gather(jnp.concatenate(lines), axis), 0, {})]
    mul x3 -> x0, other arithmetic: 18.5 us -> none  [the longest x1 18.3 us: spectra(): spectrum * values[2 * length:]]
    cos x1 -> x0, other arithmetic: 10.5 us -> none  [tables(): cosine = jnp.cos(angles)]
    sin x1 -> x0, other arithmetic: 9.06 us -> none  [tables(): sine_table = jnp.sin(angles)]
    add x6 -> x0, other arithmetic: 4.5 us -> none  [the longest x1 4.25 us: shards(): return states + jnp.exp(logs) * incoming[None, :]]
  transfers between devices with their start and end apart: 1 -> 0, of which waited for: 0 -> 0; matrix products, arithmetic and copies ran while one was open for 13% -> 0% of each run, Pallas kernels for 0% -> 0%
where the time goes in v1:
time: 64.2 us; the launch traced here: 63.9 us
  Pallas kernels  53 us (83%)
  local copies, waits for them, and re-layouts  8.79 us (14%)
  other arithmetic  2.04 us (3%)
    pallas_call x1, Pallas kernels, shards(): pl.pallas_call(functools.partial(fields, length, sections), name='fields'...  49 us
    unnamed x18, local copies, waits for them, and re-layouts  7.38 us
    pallas_call x1, Pallas kernels, shards(): pl.pallas_call(functools.partial(close, length), name='close', out_shape=...  3.95 us
    reduce_sum x1, other arithmetic, shards(): logs = jnp.broadcast_to(jnp.sum(jnp.log(sudden_shrink)), (1, 128))  1.29 us

profile of v1, /device:TPU:1, one launch (start us, length us, event | category | flops | bytes accessed | tf_op | source)
XLA Modules:
  0.0 63.9 jit_solution(16505317188720063904)
XLA Ops:
  0.0 1.3 %log_reduce_fusion = f32[]{:T(128)} fusion(f32[384]{0:T(512)} %param.9), kind=kLoop, calls=%fused_computation.6 | loop fusion | flops 383 | bytes 1540 | tf_op jit(solution)/shard_map/reduce_sum | solution.py:418
  1.3 0.6 %broadcast_in_dim.3.logs_ref = f32[1,128]{1,0:T(1,128)S(1)} broadcast(f32[]{:T(128)} %log_reduce_fusion), dimensions={} | broadcast | bytes 516 | tf_op jit(solution)/shard_map/broadcast_in_dim | solution.py:418
  1.9 0.8 %reshape.7 = f32[8,48]{1,0:T(8,128)S(1)} reshape(f32[384]{0:T(512)} %param.9) | data formatting | bytes 3072 | tf_op jit(solution)/shard_map/reshape | solution.py:417
  2.7 0.7 %negate_exponential_fusion = (f32[2048]{0:T(1024)S(1)}, f32[2048]{0:T(1024)S(1)}, f32[2048]{0:T(1024)S(1)}) fusion(f32[2048]{0:T(1024)} %param.8), kind=kLoop, calls=%fused_computation.5 | loop fusion | flops 8192 | bytes 32768 | tf_op jit(solution)/shard_map/exp | solution.py:415
  3.5 0.0 copy-start
  3.5 1.5 %copy-done = bf16[384,2304]{1,0:T(8,128)(2,1)S(1)} copy-done((bf16[384,2304]{1,0:T(8,128)(2,1)S(1)}, bf16[384,2304]{1,0:T(8,128)(2,1)}, u32[]{:S(2)}) %copy-start) | copy-done | bytes 1769496
  5.0 0.0 copy-start.1
  5.0 1.4 %copy-done.1 = bf16[384,2048]{1,0:T(8,128)(2,1)S(1)} copy-done((bf16[384,2048]{1,0:T(8,128)(2,1)S(1)}, bf16[384,2048]{1,0:T(8,128)(2,1)}, u32[]{:S(2)}) %copy-start.1) | copy-done | bytes 1572888
  6.4 0.0 copy-start.2
  6.4 1.3 %copy-done.2 = bf16[768,768]{1,0:T(8,128)(2,1)S(1)} copy-done((bf16[768,768]{1,0:T(8,128)(2,1)S(1)}, bf16[768,768]{1,0:T(8,128)(2,1)}, u32[]{:S(2)}) %copy-start.2) | copy-done | bytes 1179672
  7.6 0.0 copy-start.7
  7.6 0.7 %copy-done.7 = f32[2048]{0:T(1024)S(1)} copy-done((f32[2048]{0:T(1024)S(1)}, f32[2048]{0:T(1024)}, u32[]{:S(2)}) %copy-start.7) | copy-done | bytes 8216
  8.3 0.0 copy-start.3
  8.3 49.0 %fields.1 = (f32[16,384,128]{2,1,0:T(8,128)}, f32[16,8,128]{2,1,0:T(8,128)S(1)}, f32[16,8,128]{2,1,0:T(8,128)S(1)}, f32[384,128]{1,0:T(8,128)S(1)}, f32[16,128]{1,0:T(8,128)S(1)}) custom-call(bf16[384,2048]{1,0:T(8,128)(2,1)S(1)} %copy-done.1, f32[768,2048]{1,0:T(8,128)} %e_hbm.1, bf16[768,768]{1,0:T(8,128)(2,1)S(1)} %copy-done.2, ...), custom_call_target="tpu_custom_call" | custom-call | tf_op jit(solution)/shard_map/fields/pallas_call | solution.py:423
  57.4 0.0 copy-done.3
  57.4 0.0 copy-start.4
  57.4 0.7 %copy-done.4 = f32[384,128]{1,0:T(8,128)} copy-done((f32[384,128]{1,0:T(8,128)}, f32[384,128]{1,0:T(8,128)S(1)}, u32[]{:S(2)}) %copy-start.4) | copy-done | bytes 196632
  58.1 0.0 copy-start.5
  58.1 0.6 copy-done.5
  58.7 0.0 copy-start.6
  58.7 0.6 copy-done.6
  59.3 0.0 copy-start.8
  59.3 0.6 copy-done.8
  59.9 3.9 %close.1 = f32[384,2048]{1,0:T(8,128)} custom-call(f32[16,384,128]{2,1,0:T(8,128)} %get-tuple-element.10.x_ref, f32[16,8,128]{2,1,0:T(8,128)} %copy-done.5, f32[16,8,128]{2,1,0:T(8,128)} %copy-done.6, f32[384,128]{1,0:T(8,128)} %copy-done.4, f32[16,128]{1,0:T(8,128)} %copy-done.8, f32[8,2048]{1,0:T(8,128)} %copy-done.3), custom_call_target="tpu_custom_call" | custom-call | tf_op jit(solution)/shard_map/close/pallas_call | solution.py:488
  (2 shorter events, 0.0 us)
Async XLA Ops:
  3.5 1.5 %copy-start = (bf16[384,2304]{1,0:T(8,128)(2,1)S(1)}, bf16[384,2304]{1,0:T(8,128)(2,1)}, u32[]{:S(2)}) copy-start(bf16[384,2304]{1,0:T(8,128)(2,1)} %constant.13.clone.inverse_hbm) | copy-start | bytes 5308420
  5.0 1.4 %copy-start.1 = (bf16[384,2048]{1,0:T(8,128)(2,1)S(1)}, bf16[384,2048]{1,0:T(8,128)(2,1)}, u32[]{:S(2)}) copy-start(bf16[384,2048]{1,0:T(8,128)(2,1)} %v_hbm.1) | copy-start | bytes 4718596
  6.4 1.3 %copy-start.2 = (bf16[768,768]{1,0:T(8,128)(2,1)S(1)}, bf16[768,768]{1,0:T(8,128)(2,1)}, u32[]{:S(2)}) copy-start(bf16[768,768]{1,0:T(8,128)(2,1)} %constant.12.clone.forward_hbm) | copy-start | bytes 3538948
  7.6 0.7 %copy-start.7 = (f32[2048]{0:T(1024)S(1)}, f32[2048]{0:T(1024)}, u32[]{:S(2)}) copy-start(f32[2048]{0:T(1024)} %param.8) | copy-start | bytes 24580
  8.3 49.1 %copy-start.3 = (f32[8,2048]{1,0:T(8,128)}, f32[8,2048]{1,0:T(8,128)S(1)}, u32[]{:S(2)}) copy-start(f32[8,2048]{1,0:T(8,128)S(1)} %select_maximum_fusion.rows_ref) | copy-start | bytes 196612
  57.4 0.7 %copy-start.4 = (f32[384,128]{1,0:T(8,128)}, f32[384,128]{1,0:T(8,128)S(1)}, u32[]{:S(2)}) copy-start(f32[384,128]{1,0:T(8,128)S(1)} %get-tuple-element.13.grown_ref) | copy-start | bytes 589828
  58.1 0.6 copy-start.5
  58.7 0.6 copy-start.6
  59.3 0.6 copy-start.8

commit v2 on v1

v2 whole, which is shorter than its diff:
```python
import functools

import jax
import jax.numpy as jnp
import ml_dtypes
import numpy as np
from jax import lax
from jax.experimental import pallas as pl
from jax.experimental.pallas import tpu as pltpu
from jax.sharding import PartitionSpec as P

MESH = pl.DeviceIdType.MESH
F32 = jnp.float32
BF16 = jnp.bfloat16
MEMBERS = 16


def split(table):
    high = table.astype(ml_dtypes.bfloat16)
    low = (table - high.astype(np.float64)).astype(ml_dtypes.bfloat16)
    return high, low


@functools.lru_cache
def tables(length):
    half = length // 2
    t = np.arange(length)
    even = 2 * np.arange(half)
    odd = even + 1

    def basis(f, function):
        return function(2.0 * np.pi * (np.outer(f, t) % (2 * length)) / (2 * length))

    even_sine = basis(even, np.sin)
    even_sine[0] = np.cos(np.pi * t)
    rows = np.concatenate([basis(even, np.cos), even_sine, basis(odd, np.cos), basis(odd, np.sin)])
    forward = np.concatenate(split(rows), axis=1)
    runs = length // 8
    order = (np.arange(8)[None, :] * runs + np.arange(runs)[:, None]).reshape(-1)
    high, low = split(rows.T[order])
    parts = []
    for k in range(2):
        at = slice(k * length, (k + 1) * length)
        parts += [high[:, at], low[:, at]]
    return forward, np.concatenate(parts, axis=1)


def flipped(tile):
    at = 7 - lax.broadcasted_iota(jnp.int32, tile.shape, 0)
    return jnp.take_along_axis(tile, at, axis=0)


def fold(e_ref, es_ref, lane, length):
    half = length // 2
    scale = 1.0 / (2 * length)
    row = lax.broadcasted_iota(jnp.int32, (8, 128), 0)
    for b in range(half // 8):
        value = e_ref[lane, pl.ds(16 * b, 8, stride=2), :]
        if b:
            mirror = flipped(e_ref[lane, pl.ds(2 * length - 14 - 16 * b, 8, stride=2), :])
        else:
            mirror = flipped(e_ref[lane, pl.ds(2 * length - 16, 8, stride=2), :])
            mirror = jnp.where(row == 0, 0.0, pltpu.roll(mirror, 1, 0))
        total = (value + mirror) * scale
        es_ref[lane, 8 * b : 8 * b + 8, :] = total
        if b == 0:
            middle = jnp.broadcast_to(e_ref[lane, length : length + 1, :], (8, 128)) * scale
            total = jnp.where(row == 0, middle, total)
        es_ref[lane, half + 8 * b : half + 8 * b + 8, :] = total
        value = e_ref[lane, pl.ds(16 * b + 1, 8, stride=2), :]
        mirror = flipped(e_ref[lane, pl.ds(2 * length - 15 - 16 * b, 8, stride=2), :])
        es_ref[lane, 2 * half + 8 * b : 2 * half + 8 * b + 8, :] = (value + mirror) * -scale


def over_runs(state, decay):
    row = lax.broadcasted_iota(jnp.int32, state.shape, 0)
    for step in (1, 2, 4):
        reach = row >= step
        state = jnp.where(reach, decay * pltpu.roll(state, step, 0) + state, state)
        decay = jnp.where(reach, decay * pltpu.roll(decay, step, 0), decay)
    return state, decay


def weighted(value, loss, power, spread):
    square = loss + power * spread
    return square * lax.rsqrt(square) * value


def spread_of(rate):
    x = 2.0 * rate
    series = 1.0 - x * (1.0 / 6.0)
    for k in (5, 4, 3, 2):
        series = 1.0 - x * (1.0 / k) * series
    return x * series


def fields(
    length, sections, v_hbm, e_hbm, forward_hbm, inverse_hbm, rate_hbm, burst_hbm, x_ref,
    v_ref, e_ref, forward_ref, inverse_ref, rate_ref, burst_line, es_ref, earlier_ref, twice_ref,
    value0_ref, value1_ref, scaled0_ref, scaled1_ref, p0_ref, p1_ref, q0_ref, q1_ref, lead_ref,
    own_ref, next_ref, burst_ref, next_burst_ref, ends_ref, carry_ref, reach_ref, incoming_ref, logs_ref,
    a_ref, c_ref, pair_out_ref, pair_in_ref, before_ref, chips_ref, groups_ref,
    member_logs_ref, group_logs_ref, group_log_ref, chip_out_ref, group_out_ref, give_ref, take_ref,
    t_sem, e_sem, noise_send, noise_recv, burst_sem, pair_sem, give_sem, logs_sem, chips_sem, groups_sem, glogs_sem,
):
    width = v_hbm.shape[1]
    chunk = 256
    chunks = width // chunk
    lanes = width // 128
    half = length // 2
    runs = length // 8
    groups = sections // MEMBERS
    chips = MEMBERS // 2
    me = lax.axis_index("tm")
    group, member = me // MEMBERS, me % MEMBERS
    chip, core = member // 2, member % 2
    after, before = (me + 1) % sections, (me + sections - 1) % sections
    partner = group * MEMBERS + chip * 2 + (1 - core)
    values, scaleds = (value0_ref, value1_ref), (scaled0_ref, scaled1_ref)
    ps, qs = (p0_ref, p1_ref), (q0_ref, q1_ref)

    def remote(source, target, send, recv, device):
        return pltpu.make_async_remote_copy(
            src_ref=source, dst_ref=target, send_sem=send, recv_sem=recv, device_id={"tm": device}, device_id_type=MESH
        )

    def columns(i):
        return pl.ds(pl.multiple_of(i * chunk, chunk), chunk)

    members = [group * MEMBERS + (member + k) % MEMBERS for k in range(1, MEMBERS)]
    chip_peers = [group * MEMBERS + ((chip + k) % chips) * 2 + core for k in range(1, chips)]
    group_peers = [((group + k) % groups) * MEMBERS + member for k in range(1, groups)]

    barrier = pltpu.get_barrier_semaphore()
    for device in [after, before] + group_peers + members:
        pl.semaphore_signal(barrier, inc=1, device_id={"tm": device}, device_id_type=MESH)

    def arrived(ref, sem):
        pltpu.make_async_copy(ref, ref, sem).wait()

    for lane in range(lanes):
        pltpu.make_async_copy(e_hbm.at[:, pl.ds(lane * 128, 128)], e_ref.at[lane], e_sem.at[lane // 4]).start()
    pltpu.make_async_copy(burst_hbm, burst_line, t_sem.at[0]).start()
    for k in range(2):
        pltpu.make_async_copy(v_hbm, v_ref.at[pl.ds(k * length, length)], t_sem.at[1]).start()
    pltpu.make_async_copy(forward_hbm, forward_ref, t_sem.at[2]).start()
    for k, source in enumerate((0, 0, 1, 2, 2, 3)):
        pltpu.make_async_copy(
            inverse_hbm.at[:, pl.ds(source * length, length)], inverse_ref.at[:, pl.ds(k * length, length)], t_sem.at[3]
        ).start()
    pltpu.make_async_copy(rate_hbm, rate_ref, t_sem.at[4]).start()

    def broadcasts(source_ref, target_ref):
        product = jnp.ones((8, 128), F32)
        for j in range(runs):
            column = jnp.broadcast_to(source_ref[:, j : j + 1], (8, 128))
            at = slice(8 * j, 8 * j + 8)
            power = column * column
            target_ref[0, at, :] = column
            target_ref[1, at, :] = 1.0 - power
            target_ref[2, at, :] = power
            product = product * column
            if source_ref is burst_ref:
                x_ref[lanes, 8 * j : 8 * j + 8, :] = product
        return product

    def noise(i):
        return remote(v_hbm.at[:, columns(i)], earlier_ref.at[:, columns(i)], noise_send.at[0], noise_recv.at[i], after)

    burst_copy = remote(burst_ref, next_burst_ref, burst_sem.at[0], burst_sem.at[1], before)

    def fold_step(lane, carry):
        @pl.when(lane % 4 == 0)
        def _():
            four = e_ref.at[pl.ds(pl.multiple_of(lane, 4), 4)]
            arrived(four, e_sem.at[lane // 4])

        fold(e_ref, es_ref, lane, length)
        return carry

    lax.fori_loop(0, lanes // 2, fold_step, 0)
    arrived(burst_line, t_sem.at[0])
    line = jnp.concatenate([burst_line[k : k + 1, :] for k in range(length // 128)], axis=1)
    burst_ref[:, 0:runs] = jnp.concatenate([line[:, runs * k : runs * k + runs] for k in range(8)], axis=0)
    burst_ref[:, runs:128] = jnp.ones((8, 128 - runs), F32)
    logs_ref[...] = jnp.broadcast_to(jnp.sum(jnp.log(line), axis=1, keepdims=True), (1, 128))

    pl.semaphore_wait(barrier, 2 + (MEMBERS - 1) + (groups - 1))
    burst_copy.start()
    noise(0).start()
    noise(1).start()
    for device in members:
        remote(logs_ref, member_logs_ref.at[member], logs_sem.at[0], logs_sem.at[1], device).start()

    ends_ref[0] = broadcasts(burst_ref, own_ref)
    lax.fori_loop(lanes // 2, lanes, fold_step, 0)
    for k, ref in ((4, rate_ref), (1, v_ref), (2, forward_ref), (3, inverse_ref)):
        arrived(ref, t_sem.at[k])
    x_ref[lanes + 1, 0:lanes, :] = rate_ref[...]

    def rate_rows(lane):
        rate = jnp.broadcast_to(rate_ref[pl.ds(lane, 1), :], (8, 128))
        return jnp.exp(-rate), jnp.exp(-runs * rate), spread_of(rate)

    def forward(data, slot, part):
        at = slice(half * part, half * part + half)
        values[slot][at, :] = jnp.dot(forward_ref[at, :], data, preferred_element_type=F32)

    def scale(i, slot, part):
        at = (0, half, 2 * half, 2 * half)[part]
        base = 3 * length * (part // 2) + half * (part % 2)
        for side in range(2):
            cut = slice(128 * side, 128 * side + 128)
            scaled = values[slot][half * part : half * part + half, cut] * es_ref[2 * i + side, at : at + half, :]
            high = scaled.astype(BF16)
            low = (scaled - high.astype(F32)).astype(BF16)
            scaleds[slot][base : base + half, cut] = high
            scaleds[slot][base + length : base + length + half, cut] = low
            scaleds[slot][base + 2 * length : base + 2 * length + half, cut] = high

    def early_inverse(slot, part):
        target, cut = (ps, qs)[part // 2], slice(3 * length * (part // 2), 3 * length * (part // 2) + 3 * length)
        at = slice(half * (part % 2), half * (part % 2) + half)
        target[slot][at, :] = jnp.dot(inverse_ref[at, cut], scaleds[slot][cut, :], preferred_element_type=F32)

    def early_scan(i, slot, states, piece, pieces):
        for side in range(2):
            lane = 2 * i + side
            if piece == 0:
                states[side] = rate_rows(lane) + (jnp.zeros((8, 128), F32), jnp.zeros((8, 128), F32))
            keep, keep_run, spread, here, there = states[side]
            for j in range(runs * piece // pieces, runs * (piece + 1) // pieces):
                at = slice(8 * j, 8 * j + 8)
                p = ps[slot][at, 128 * side : 128 * side + 128]
                q = qs[slot][at, 128 * side : 128 * side + 128]
                lead = p - q
                lead_ref[lane, at, :] = lead
                force = weighted(lead, own_ref[1, at, :], own_ref[2, at, :], spread)
                here = (own_ref[0, at, :] * keep) * here + force
                force = weighted(p + q, next_ref[1, at, :], next_ref[2, at, :], spread)
                there = (next_ref[0, at, :] * keep) * there + force
            states[side] = (keep, keep_run, spread, here, there)
            if piece < pieces - 1:
                continue
            here, _ = over_runs(here, ends_ref[0] * keep_run)
            there, _ = over_runs(there, ends_ref[1] * keep_run)
            a_ref[pl.ds(lane, 1), :] = here[7:8, :]
            c_ref[pl.ds(lane, 1), :] = there[7:8, :]

    def whole(scan, i, slot):
        scan(i, slot, [None, None], 0, 1)

    def step(i, slot, data, inverse, scan):
        states = [None, None]
        for part in range(4):
            forward(data, 1 - slot, part)
            scan((i + chunks - 1) % chunks, 1 - slot, states, part, 8)
        for part in range(4):
            inverse(slot, part)
            scale(i + 1, 1 - slot, part)
            scan((i + chunks - 1) % chunks, 1 - slot, states, part + 4, 8)

    def early_step(i, slot):
        step(i, slot, v_ref[:, columns(i + 1)], early_inverse, early_scan)

    for part in range(4):
        forward(v_ref[:, columns(0)], 0, part)
        scale(0, 0, part)
    def early_pair(u, carry):
        noise(2 + u).start()
        early_step(2 * u, 0)

        @pl.when(u == 0)
        def _():
            burst_copy.wait()
            ends_ref[1] = broadcasts(next_burst_ref, next_ref)

        early_step(2 * u + 1, 1)
        return carry

    lax.fori_loop(0, chunks // 2 - 1, early_pair, 0)
    noise(chunks // 2 + 1).start()
    early_step(chunks - 2, 0)
    states = [None, None]
    for part in range(4):
        early_inverse(1, part)
        early_scan(chunks - 2, 0, states, part, 4)
    whole(early_scan, chunks - 1, 1)
    sent_early = chunks // 2 + 2

    own_half = pl.ds(pl.multiple_of(core * 8, 8), 8)
    other_half = pl.ds(pl.multiple_of((1 - core) * 8, 8), 8)
    pair_copy = remote(pair_out_ref, pair_in_ref, pair_sem.at[0], pair_sem.at[1], partner)
    give_copy = remote(give_ref, take_ref, give_sem.at[0], give_sem.at[1], partner)
    pair_out_ref[0] = a_ref[other_half, :]
    pair_out_ref[1] = c_ref[other_half, :]
    pair_copy.start()

    for k in range(2):
        arrived(member_logs_ref.at[pl.ds(0, MEMBERS - 1)], logs_sem.at[k])
    member_logs_ref[pl.ds(member, 1)] = logs_ref[...].reshape(1, 1, 128)
    logs_of = [member_logs_ref[k] for k in range(MEMBERS)]
    group_log_ref[0:1, :] = sum(logs_of[1:], logs_of[0])
    group_log_ref[1:2, :] = logs_of[0]
    group_logs_ref[pl.ds(group, 1)] = group_log_ref[...].reshape(1, 2, 128)
    for device in group_peers:
        remote(group_log_ref, group_logs_ref.at[group], glogs_sem.at[0], glogs_sem.at[1], device).start()

    def log_of(index):
        return jnp.broadcast_to(member_logs_ref[index], (8, 128)) - length * rate_ref[own_half, :]

    def of_first(k):
        own = (a_ref, c_ref)[k][own_half, :]
        return jnp.where(core == 0, own, pair_in_ref[k])

    def of_second(k):
        own = (a_ref, c_ref)[k][own_half, :]
        return jnp.where(core == 0, pair_in_ref[k], own)

    def exchange_chips():
        pair_copy.wait()
        chip_out_ref[0] = jnp.exp(log_of(2 * chip + 1)) * of_first(0) + of_first(1) + of_second(0)
        chip_out_ref[1] = of_second(1)
        for device in chip_peers:
            remote(chip_out_ref, chips_ref.at[chip], chips_sem.at[0], chips_sem.at[1], device).start()
        chips_ref[pl.ds(chip, 1)] = chip_out_ref[...].reshape(1, 2, 8, 128)

    def exchange_groups():
        for k in range(2):
            arrived(chips_ref.at[pl.ds(0, chips - 1)], chips_sem.at[k])
        state = jnp.zeros((8, 128), F32)
        log, tail = state, state
        before = (state, log, tail)
        for k in range(chips):
            here = chip == k
            before = tuple(jnp.where(here, new, old) for new, old in zip((state, log, tail), before))
            second = log_of(2 * k + 1)
            step = log_of(2 * k) + second
            state = jnp.exp(step) * state + jnp.exp(second) * tail + chips_ref[k, 0]
            tail = chips_ref[k, 1]
            log = log + step
        group_out_ref[0] = state
        group_out_ref[1] = tail
        for device in group_peers:
            remote(group_out_ref, groups_ref.at[group], groups_sem.at[0], groups_sem.at[1], device).start()
        groups_ref[pl.ds(group, 1)] = group_out_ref[...].reshape(1, 2, 8, 128)
        for k in range(3):
            before_ref[k] = before[k]

    def exchange_back():
        for k in range(2):
            arrived(groups_ref.at[pl.ds(0, groups - 1)], groups_sem.at[k])
        for k in range(2):
            arrived(group_logs_ref.at[pl.ds(0, groups - 1)], glogs_sem.at[k])
        rate = rate_ref[own_half, :]
        entering = groups_ref[(group + groups - 1) % groups, 1]
        state = jnp.zeros((8, 128), F32)
        log, tail = state, entering
        for k in range(groups):
            at = (group + k) % groups
            total = jnp.broadcast_to(group_logs_ref[at, 0:1, :], (8, 128))
            first = jnp.broadcast_to(group_logs_ref[at, 1:2, :], (8, 128))
            step = total - (MEMBERS * length) * rate
            rest = (total - first) - ((MEMBERS - 1) * length) * rate
            state = jnp.exp(step) * state + jnp.exp(rest) * tail + groups_ref[at, 0]
            tail = groups_ref[at, 1]
            log = log + step
        opening = state / (1.0 - jnp.exp(log))
        log = before_ref[1]
        arriving = jnp.where(chip == 0, 0.0, jnp.exp(log - log_of(0)) * entering)
        first_in = jnp.exp(log) * opening + before_ref[0] + arriving
        tail = jnp.where(chip == 0, entering, before_ref[2])
        second_in = jnp.exp(log_of(2 * chip)) * first_in + of_first(0) + tail
        incoming_ref[own_half, :] = jnp.where(core == 0, first_in, second_in)
        give_ref[...] = jnp.where(core == 0, second_in, first_in)
        give_copy.start()

    def arrive(i):
        noise(i).wait_recv()

    def late_data(i):
        block = earlier_ref[:, columns(i)]
        twice_ref[0:length, :] = block
        twice_ref[length : 2 * length, :] = block
        return twice_ref[...]

    def late_inverse(slot, part):
        at = slice(half * part, half * part + half)
        if part < 2:
            ps[slot][at, :] = jnp.dot(inverse_ref[at, :], scaleds[slot][...], preferred_element_type=F32)

    def late_scan(i, slot, states, piece, pieces):
        for side in range(2):
            lane = 2 * i + side
            if piece == 0:
                states[side] = rate_rows(lane) + (jnp.zeros((8, 128), F32),)
            keep, keep_run, spread, state = states[side]
            for j in range(runs * piece // pieces, runs * (piece + 1) // pieces):
                at = slice(8 * j, 8 * j + 8)
                series = lead_ref[lane, at, :] + ps[slot][at, 128 * side : 128 * side + 128]
                force = weighted(series, own_ref[1, at, :], own_ref[2, at, :], spread)
                state = (own_ref[0, at, :] * keep) * state + force
                x_ref[lane, at, :] = state
            states[side] = (keep, keep_run, spread, state)
            if piece < pieces - 1:
                continue
            state, decay = over_runs(state, ends_ref[0] * keep_run)
            row = lax.broadcasted_iota(jnp.int32, (8, 128), 0)
            carry_ref[lane] = jnp.where(row == 0, 0.0, pltpu.roll(state, 1, 0))
            reach_ref[lane] = jnp.where(row == 0, 1.0, pltpu.roll(decay, 1, 0))

    def late_step(i, slot):
        step(i, slot, late_data(i + 1), late_inverse, late_scan)

    noise(sent_early).start()
    arrive(0)
    first_data = late_data(0)
    for part in range(4):
        forward(first_data, 0, part)
        scale(0, 0, part)

    def late_pair(u, carry):
        arrive(2 * u + 1)
        late_step(2 * u, 0)

        @pl.when(u == 0)
        def _():
            exchange_chips()
            noise(sent_early + 1).start()

        pl.when(u == 2)(exchange_groups)
        arrive(2 * u + 2)
        late_step(2 * u + 1, 1)
        return carry

    lax.fori_loop(0, chunks // 2 - 1, late_pair, 0)
    arrive(chunks - 1)
    late_step(chunks - 2, 0)
    states = [None, None]
    for part in range(2):
        late_inverse(1, part)
        late_scan(chunks - 2, 0, states, part, 2)
    exchange_back()
    whole(late_scan, chunks - 1, 1)
    give_copy.wait()
    incoming_ref[other_half, :] = take_ref[...]
    for lane in range(lanes):
        incoming = jnp.broadcast_to(incoming_ref[lane : lane + 1, :], (8, 128))
        x_ref[lane, length : length + 8, :] = carry_ref[lane] + reach_ref[lane] * incoming

    arrived(earlier_ref, noise_send.at[0])


def close(length, x_ref, out_hbm, stage_ref, sem):
    lanes = stage_ref.shape[0]
    runs = length // 8

    def out(lane):
        return pltpu.make_async_copy(
            stage_ref.at[lane], out_hbm.at[:, pl.ds(pl.multiple_of(lane * 128, 128), 128)], sem.at[lane]
        )

    def step(lane, carry):
        keep = jnp.exp(-jnp.broadcast_to(x_ref[lanes + 1, pl.ds(lane, 1), :], (8, 128)))
        state = x_ref[lane, length : length + 8, :] * keep
        for j in range(runs):
            at = slice(8 * j, 8 * j + 8)
            stage_ref[lane, pl.ds(j, 8, stride=runs), :] = x_ref[lane, at, :] + x_ref[lanes, at, :] * state
            state = state * keep
        out(lane).start()
        return carry

    lax.fori_loop(0, lanes, step, 0)

    def drain(lane, carry):
        out(lane).wait()
        return carry

    lax.fori_loop(0, lanes, drain, 0)


def shards(sections, random_forcing, eigen_root_table, lane_fading_speed, sudden_shrink):
    length, width = random_forcing.shape
    lanes, half = width // 128, length // 2
    chunk = 256
    chunks = width // chunk
    groups, chips = sections // MEMBERS, MEMBERS // 2
    forward, inverse = tables(length)
    hbm = pl.BlockSpec(memory_space=pltpu.HBM)
    vmem = pl.BlockSpec(memory_space=pltpu.VMEM)
    dma = pltpu.SemaphoreType.DMA
    tile = pltpu.VMEM((8, 128), F32)
    dense = pltpu.VMEM((lanes, 128), F32)
    x = pl.pallas_call(
        functools.partial(fields, length, sections),
        name="fields",
        out_shape=pltpu.VMEM((lanes + 2, length + 8, 128), F32),
        in_specs=[hbm] * 6,
        out_specs=vmem,
        scratch_shapes=[
            pltpu.VMEM((2 * length, width), BF16),
            pltpu.VMEM((lanes, 2 * length, 128), F32),
            pltpu.VMEM((2 * length, 2 * length), BF16),
            pltpu.VMEM((length, 6 * length), BF16),
            dense,
            pltpu.VMEM((length // 128, 128), F32),
            pltpu.VMEM((lanes, 3 * half, 128), F32),
            pltpu.VMEM((length, width), BF16),
            pltpu.VMEM((2 * length, chunk), BF16),
            pltpu.VMEM((2 * length, chunk), F32),
            pltpu.VMEM((2 * length, chunk), F32),
            pltpu.VMEM((6 * length, chunk), BF16),
            pltpu.VMEM((6 * length, chunk), BF16),
            pltpu.VMEM((length, chunk), F32),
            pltpu.VMEM((length, chunk), F32),
            pltpu.VMEM((length, chunk), F32),
            pltpu.VMEM((length, chunk), F32),
            pltpu.VMEM((lanes, length, 128), F32),
            pltpu.VMEM((3, length, 128), F32),
            pltpu.VMEM((3, length, 128), F32),
            tile,
            tile,
            pltpu.VMEM((2, 8, 128), F32),
            pltpu.VMEM((lanes, 8, 128), F32),
            pltpu.VMEM((lanes, 8, 128), F32),
            dense,
            pltpu.VMEM((1, 128), F32),
            dense,
            dense,
            pltpu.VMEM((2, 8, 128), F32),
            pltpu.VMEM((2, 8, 128), F32),
            pltpu.VMEM((3, 8, 128), F32),
            pltpu.VMEM((chips, 2, 8, 128), F32),
            pltpu.VMEM((groups, 2, 8, 128), F32),
            pltpu.VMEM((MEMBERS, 1, 128), F32),
            pltpu.VMEM((groups, 2, 128), F32),
            pltpu.VMEM((2, 128), F32),
            pltpu.VMEM((2, 8, 128), F32),
            pltpu.VMEM((2, 8, 128), F32),
            tile,
            tile,
            dma((5,)),
            dma((lanes // 4,)),
            dma((1,)),
            dma((chunks,)),
        ]
        + [dma((2,))] * 7,
        compiler_params=pltpu.CompilerParams(
            collective_id=0, has_side_effects=True, vmem_limit_bytes=44 * 2**20
        ),
    )(
        *(
            pltpu.with_memory_space_constraint(operand, pltpu.HBM)
            for operand in (
                random_forcing,
                eigen_root_table,
                jnp.asarray(forward),
                jnp.asarray(inverse),
                lane_fading_speed.reshape(lanes, 128),
                sudden_shrink.reshape(length // 128, 128),
            )
        )
    )
    return pl.pallas_call(
        functools.partial(close, length),
        name="close",
        out_shape=jax.ShapeDtypeStruct((length, width), F32),
        in_specs=[vmem],
        out_specs=hbm,
        scratch_shapes=[pltpu.VMEM((lanes, length, 128), F32), dma((lanes,))],
        compiler_params=pltpu.CompilerParams(vmem_limit_bytes=8 * 2**20),
    )(x)


def solution(mesh):
    return jax.shard_map(
        functools.partial(shards, mesh.shape["tm"]),
        mesh=mesh,
        in_specs=(P("tm", "chan"), P(None, "chan"), P("chan"), P("tm")),
        out_specs=P("tm", "chan"),
        check_vma=False,
    )
```

time: 64.2 us -> 40.7 us (0.63)
  Pallas kernels: 53 us -> 40.6 us
  local copies, waits for them, and re-layouts: 8.79 us -> 0 us
  other arithmetic: 2.04 us -> 0 us
    pallas_call x1, Pallas kernels: 49 us -> 38.5 us  [shards(): pl.pallas_call(functools.partial(fields, length, sections), name='fields'...]
    unnamed x18 -> x0, local copies, waits for them, and re-layouts: 7.38 us -> none
    pallas_call x1, Pallas kernels: 3.95 us -> 2.03 us  [shards(): pl.pallas_call(functools.partial(close, length), name='close', out_shape=...]
    reduce_sum x1 -> x0, other arithmetic: 1.29 us -> none  [shards(): logs = jnp.broadcast_to(jnp.sum(jnp.log(sudden_shrink)), (1, 128))]
    reshape x1 -> x0, local copies, waits for them, and re-layouts: 0.76 us -> none  [shards(): burst = jnp.pad(sudden_shrink.reshape(8, runs), ((0, 0), (0, 128 - runs)))]
    exp x1 -> x0, other arithmetic: 0.71 us -> none  [shards(): jnp.exp(-rate)]
    broadcast_in_dim x1 -> x0, local copies, waits for them, and re-layouts: 0.65 us -> none  [shards(): logs = jnp.broadcast_to(jnp.sum(jnp.log(sudden_shrink)), (1, 128))]
where the time goes in v2:
time: 40.7 us; the launch traced here: 40.6 us
  Pallas kernels  40.6 us (100%)
    pallas_call x1, Pallas kernels, shards(): pl.pallas_call(functools.partial(fields, length, sections), name='fields'...  38.5 us
    pallas_call x1, Pallas kernels, shards(): pl.pallas_call(functools.partial(close, length), name='close', out_shape=...  2.03 us

profile of v2, /device:TPU:1, one launch (start us, length us, event | category | flops | bytes accessed | tf_op | source)
XLA Modules:
  0.0 40.6 jit_solution(11042961187687913783)
XLA Ops:
  0.0 38.5 %fields.1.x_ref = f32[18,392,128]{2,1,0:T(8,128)S(1)} custom-call(bf16[384,2048]{1,0:T(8,128)(2,1)} %v_hbm.1, f32[768,2048]{1,0:T(8,128)} %e_hbm.1, bf16[768,768]{1,0:T(8,128)(2,1)} %constant.4.clone.forward_hbm, bf16[384,1536]{1,0:T(8,128)(2,1)} %constant.5.clone.inverse_hbm, f32[16,128]{1,0:T(8,128)} %bitcast.2, f32[3,128]{1,0:T(4,128)} %bitcast.3), custom_call_target="tpu_custom_call" | custom-call | tf_op jit(solution)/shard_map/fields/pallas_call | solution.py:494
  38.6 2.0 %close.1 = f32[384,2048]{1,0:T(8,128)} custom-call(f32[18,392,128]{2,1,0:T(8,128)S(1)} %fields.1.x_ref), custom_call_target="tpu_custom_call" | custom-call | tf_op jit(solution)/shard_map/close/pallas_call | solution.py:564

commit v3 on v2

--- a/solution.py
+++ b/solution.py
@@ -50,11 +50,12 @@
     return jnp.take_along_axis(tile, at, axis=0)
 
 
-def fold(e_ref, es_ref, lane, length):
+def fold(e_ref, es_ref, lane, length, piece, pieces):
     half = length // 2
     scale = 1.0 / (2 * length)
     row = lax.broadcasted_iota(jnp.int32, (8, 128), 0)
-    for b in range(half // 8):
+    blocks = half // 8
+    for b in range(blocks * piece // pieces, blocks * (piece + 1) // pieces):
         value = e_ref[lane, pl.ds(16 * b, 8, stride=2), :]
         if b:
             mirror = flipped(e_ref[lane, pl.ds(2 * length - 14 - 16 * b, 8, stride=2), :])
@@ -138,17 +139,19 @@
     def arrived(ref, sem):
         pltpu.make_async_copy(ref, ref, sem).wait()
 
-    for lane in range(lanes):
-        pltpu.make_async_copy(e_hbm.at[:, pl.ds(lane * 128, 128)], e_ref.at[lane], e_sem.at[lane // 4]).start()
+    def table(lane):
+        return pltpu.make_async_copy(e_hbm.at[:, pl.ds(lane * 128, 128)], e_ref.at[lane], e_sem.at[lane // 4])
+
+    for lane in range(4):
+        table(lane).start()
     pltpu.make_async_copy(burst_hbm, burst_line, t_sem.at[0]).start()
-    for k in range(2):
-        pltpu.make_async_copy(v_hbm, v_ref.at[pl.ds(k * length, length)], t_sem.at[1]).start()
+    pltpu.make_async_copy(rate_hbm, rate_ref, t_sem.at[4]).start()
+    pltpu.make_async_copy(v_hbm, v_ref, t_sem.at[1]).start()
     pltpu.make_async_copy(forward_hbm, forward_ref, t_sem.at[2]).start()
     for k, source in enumerate((0, 0, 1, 2, 2, 3)):
         pltpu.make_async_copy(
             inverse_hbm.at[:, pl.ds(source * length, length)], inverse_ref.at[:, pl.ds(k * length, length)], t_sem.at[3]
         ).start()
-    pltpu.make_async_copy(rate_hbm, rate_ref, t_sem.at[4]).start()
 
     def broadcasts(source_ref, target_ref):
         product = jnp.ones((8, 128), F32)
@@ -170,15 +173,9 @@
     burst_copy = remote(burst_ref, next_burst_ref, burst_sem.at[0], burst_sem.at[1], before)
 
     def fold_step(lane, carry):
-        @pl.when(lane % 4 == 0)
-        def _():
-            four = e_ref.at[pl.ds(pl.multiple_of(lane, 4), 4)]
-            arrived(four, e_sem.at[lane // 4])
-
-        fold(e_ref, es_ref, lane, length)
+        fold(e_ref, es_ref, lane, length, 0, 1)
         return carry
 
-    lax.fori_loop(0, lanes // 2, fold_step, 0)
     arrived(burst_line, t_sem.at[0])
     line = jnp.concatenate([burst_line[k : k + 1, :] for k in range(length // 128)], axis=1)
     burst_ref[:, 0:runs] = jnp.concatenate([line[:, runs * k : runs * k + runs] for k in range(8)], axis=0)
@@ -187,20 +184,29 @@
 
     pl.semaphore_wait(barrier, 2 + (MEMBERS - 1) + (groups - 1))
     burst_copy.start()
-    noise(0).start()
-    noise(1).start()
     for device in members:
         remote(logs_ref, member_logs_ref.at[member], logs_sem.at[0], logs_sem.at[1], device).start()
+    for i in range(4):
+        noise(i).start()
+    for lane in range(4, 8):
+        table(lane).start()
 
     ends_ref[0] = broadcasts(burst_ref, own_ref)
-    lax.fori_loop(lanes // 2, lanes, fold_step, 0)
-    for k, ref in ((4, rate_ref), (1, v_ref), (2, forward_ref), (3, inverse_ref)):
+    arrived(e_ref.at[pl.ds(0, 4)], e_sem.at[0])
+    lax.fori_loop(0, 4, fold_step, 0)
+    for k, ref in ((4, rate_ref), (1, v_ref), (2, forward_ref)):
         arrived(ref, t_sem.at[k])
     x_ref[lanes + 1, 0:lanes, :] = rate_ref[...]
 
     def rate_rows(lane):
         rate = jnp.broadcast_to(rate_ref[pl.ds(lane, 1), :], (8, 128))
         return jnp.exp(-rate), jnp.exp(-runs * rate), spread_of(rate)
+
+    def doubled(source_ref, i):
+        block = source_ref[:, columns(i)]
+        twice_ref[0:length, :] = block
+        twice_ref[length : 2 * length, :] = block
+        return twice_ref[...]
 
     def forward(data, slot, part):
         at = slice(half * part, half * part + half)
@@ -250,43 +256,57 @@
     def whole(scan, i, slot):
         scan(i, slot, [None, None], 0, 1)
 
-    def step(i, slot, data, inverse, scan):
+    def step(i, slot, data, inverse, scan, folding=None):
         states = [None, None]
         for part in range(4):
             forward(data, 1 - slot, part)
             scan((i + chunks - 1) % chunks, 1 - slot, states, part, 8)
+            if folding is not None:
+                fold(e_ref, es_ref, folding, length, part, 4)
         for part in range(4):
             inverse(slot, part)
             scale(i + 1, 1 - slot, part)
             scan((i + chunks - 1) % chunks, 1 - slot, states, part + 4, 8)
-
-    def early_step(i, slot):
-        step(i, slot, v_ref[:, columns(i + 1)], early_inverse, early_scan)
-
+            if folding is not None:
+                fold(e_ref, es_ref, folding + 1, length, part, 4)
+
+    def early_step(i, slot, folding=None):
+        step(i, slot, doubled(v_ref, i + 1), early_inverse, early_scan, folding)
+
+    first_data = doubled(v_ref, 0)
     for part in range(4):
-        forward(v_ref[:, columns(0)], 0, part)
+        forward(first_data, 0, part)
         scale(0, 0, part)
+    arrived(inverse_ref, t_sem.at[3])
     def early_pair(u, carry):
-        noise(2 + u).start()
-        early_step(2 * u, 0)
+        noise(4 + u).start()
+        arrived(e_ref.at[pl.ds(pl.multiple_of(4 * u + 4, 4), 4)], e_sem.at[u + 1])
+
+        @pl.when(u == 0)
+        def _():
+            for lane in range(8, lanes):
+                table(lane).start()
+
+        early_step(2 * u, 0, 4 * u + 4)
+
+        early_step(2 * u + 1, 1, 4 * u + 6)
 
         @pl.when(u == 0)
         def _():
             burst_copy.wait()
             ends_ref[1] = broadcasts(next_burst_ref, next_ref)
-
-        early_step(2 * u + 1, 1)
+            whole(early_scan, 0, 0)
+
         return carry
 
     lax.fori_loop(0, chunks // 2 - 1, early_pair, 0)
-    noise(chunks // 2 + 1).start()
     early_step(chunks - 2, 0)
     states = [None, None]
     for part in range(4):
         early_inverse(1, part)
         early_scan(chunks - 2, 0, states, part, 4)
     whole(early_scan, chunks - 1, 1)
-    sent_early = chunks // 2 + 2
+    sent_early = chunks // 2 + 3
 
     own_half = pl.ds(pl.multiple_of(core * 8, 8), 8)
     other_half = pl.ds(pl.multiple_of((1 - core) * 8, 8), 8)
@@ -378,12 +398,6 @@
     def arrive(i):
         noise(i).wait_recv()
 
-    def late_data(i):
-        block = earlier_ref[:, columns(i)]
-        twice_ref[0:length, :] = block
-        twice_ref[length : 2 * length, :] = block
-        return twice_ref[...]
-
     def late_inverse(slot, part):
         at = slice(half * part, half * part + half)
         if part < 2:
@@ -410,11 +424,10 @@
             reach_ref[lane] = jnp.where(row == 0, 1.0, pltpu.roll(decay, 1, 0))
 
     def late_step(i, slot):
-        step(i, slot, late_data(i + 1), late_inverse, late_scan)
-
-    noise(sent_early).start()
+        step(i, slot, doubled(earlier_ref, i + 1), late_inverse, late_scan)
+
     arrive(0)
-    first_data = late_data(0)
+    first_data = doubled(earlier_ref, 0)
     for part in range(4):
         forward(first_data, 0, part)
         scale(0, 0, part)
@@ -426,7 +439,7 @@
         @pl.when(u == 0)
         def _():
             exchange_chips()
-            noise(sent_early + 1).start()
+            noise(sent_early).start()
 
         pl.when(u == 2)(exchange_groups)
         arrive(2 * u + 2)
@@ -434,14 +447,22 @@
         return carry
 
     lax.fori_loop(0, chunks // 2 - 1, late_pair, 0)
+    states = [None, None]
+    for part in range(2):
+        late_inverse(0, part)
+        late_scan(chunks - 3, 1, states, part, 2)
+    whole(late_scan, chunks - 2, 0)
     arrive(chunks - 1)
-    late_step(chunks - 2, 0)
+    last_data = doubled(earlier_ref, chunks - 1)
+    for part in range(4):
+        forward(last_data, 1, part)
+        scale(chunks - 1, 1, part)
+    exchange_back()
     states = [None, None]
     for part in range(2):
         late_inverse(1, part)
-        late_scan(chunks - 2, 0, states, part, 2)
-    exchange_back()
-    whole(late_scan, chunks - 1, 1)
+    for part in range(2):
+        late_scan(chunks - 1, 1, states, part, 2)
     give_copy.wait()
     incoming_ref[other_half, :] = take_ref[...]
     for lane in range(lanes):
@@ -454,29 +475,33 @@
 def close(length, x_ref, out_hbm, stage_ref, sem):
     lanes = stage_ref.shape[0]
     runs = length // 8
+    spread_ref = stage_ref.reshape(lanes, 8 * (runs + 8), 128)
 
     def out(lane):
         return pltpu.make_async_copy(
-            stage_ref.at[lane], out_hbm.at[:, pl.ds(pl.multiple_of(lane * 128, 128), 128)], sem.at[lane]
+            stage_ref.at[lane, :, pl.ds(0, runs)],
+            out_hbm.at[:, :, pl.ds(pl.multiple_of(lane * 128, 128), 128)],
+            sem.at[0],
         )
 
-    def step(lane, carry):
-        keep = jnp.exp(-jnp.broadcast_to(x_ref[lanes + 1, pl.ds(lane, 1), :], (8, 128)))
-        state = x_ref[lane, length : length + 8, :] * keep
+    def step(pair, carry):
+        both = (2 * pair, 2 * pair + 1)
+        keep = [jnp.exp(-jnp.broadcast_to(x_ref[lanes + 1, pl.ds(lane, 1), :], (8, 128))) for lane in both]
+        state = [x_ref[lane, length : length + 8, :] * k for lane, k in zip(both, keep)]
         for j in range(runs):
             at = slice(8 * j, 8 * j + 8)
-            stage_ref[lane, pl.ds(j, 8, stride=runs), :] = x_ref[lane, at, :] + x_ref[lanes, at, :] * state
-            state = state * keep
-        out(lane).start()
+            grown = x_ref[lanes, at, :]
+            for side, lane in enumerate(both):
+                spread_ref[lane, pl.ds(j, 8, stride=runs + 8), :] = x_ref[lane, at, :] + grown * state[side]
+                state[side] = state[side] * keep[side]
+        for lane in both:
+            out(lane).start()
         return carry
 
-    lax.fori_loop(0, lanes, step, 0)
-
-    def drain(lane, carry):
-        out(lane).wait()
-        return carry
-
-    lax.fori_loop(0, lanes, drain, 0)
+    lax.fori_loop(0, lanes // 2, step, 0)
+
+    written = stage_ref.at[:, :, pl.ds(0, runs)]
+    pltpu.make_async_copy(written, written, sem.at[0]).wait()
 
 
 def shards(sections, random_forcing, eigen_root_table, lane_fading_speed, sudden_shrink):
@@ -498,7 +523,7 @@
         in_specs=[hbm] * 6,
         out_specs=vmem,
         scratch_shapes=[
-            pltpu.VMEM((2 * length, width), BF16),
+            pltpu.VMEM((length, width), BF16),
             pltpu.VMEM((lanes, 2 * length, 128), F32),
             pltpu.VMEM((2 * length, 2 * length), BF16),
             pltpu.VMEM((length, 6 * length), BF16),
@@ -564,12 +589,12 @@
     return pl.pallas_call(
         functools.partial(close, length),
         name="close",
-        out_shape=jax.ShapeDtypeStruct((length, width), F32),
+        out_shape=jax.ShapeDtypeStruct((8, length // 8, width), F32),
         in_specs=[vmem],
         out_specs=hbm,
-        scratch_shapes=[pltpu.VMEM((lanes, length, 128), F32), dma((lanes,))],
+        scratch_shapes=[pltpu.VMEM((lanes, 8, length // 8 + 8, 128), F32), dma((1,))],
         compiler_params=pltpu.CompilerParams(vmem_limit_bytes=8 * 2**20),
-    )(x)
+    )(x).reshape(length, width)
 
 
 def solution(mesh):

time: 40.7 us -> 37.4 us (0.919)
  Pallas kernels: 40.6 us -> 37.3 us
    pallas_call x1, Pallas kernels: 38.5 us -> 35.6 us  [shards(): pl.pallas_call(functools.partial(fields, length, sections), name='fields'...]
where the time goes in v3:
time: 37.4 us; the launch traced here: 37.3 us
  Pallas kernels  37.3 us (100%)
    pallas_call x1, Pallas kernels, shards(): pl.pallas_call(functools.partial(fields, length, sections), name='fields'...  35.6 us
    pallas_call x1, Pallas kernels, shards(): pl.pallas_call(functools.partial(close, length), name='close', out_shape=...  1.72 us

profile of v3, /device:TPU:1, one launch (start us, length us, event | category | flops | bytes accessed | tf_op | source)
XLA Modules:
  0.0 37.3 jit_solution(16531696114935800217)
XLA Ops:
  0.0 35.6 %fields.1.x_ref = f32[18,392,128]{2,1,0:T(8,128)S(1)} custom-call(bf16[384,2048]{1,0:T(8,128)(2,1)} %v_hbm.1, f32[768,2048]{1,0:T(8,128)} %e_hbm.1, bf16[768,768]{1,0:T(8,128)(2,1)} %constant.4.clone.forward_hbm, bf16[384,1536]{1,0:T(8,128)(2,1)} %constant.5.clone.inverse_hbm, f32[16,128]{1,0:T(8,128)} %bitcast.3, f32[3,128]{1,0:T(4,128)} %bitcast.4), custom_call_target="tpu_custom_call" | custom-call | tf_op jit(solution)/shard_map/fields/pallas_call | solution.py:519
  35.6 1.7 %close.1 = f32[8,48,2048]{2,1,0:T(8,128)} custom-call(f32[18,392,128]{2,1,0:T(8,128)S(1)} %fields.1.x_ref), custom_call_target="tpu_custom_call" | custom-call | tf_op jit(solution)/shard_map/close/pallas_call | solution.py:589

commit v4 on v3

--- a/solution.py
+++ b/solution.py
@@ -98,7 +98,7 @@
 def fields(
     length, sections, v_hbm, e_hbm, forward_hbm, inverse_hbm, rate_hbm, burst_hbm, x_ref,
     v_ref, e_ref, forward_ref, inverse_ref, rate_ref, burst_line, es_ref, earlier_ref, twice_ref,
-    value0_ref, value1_ref, scaled0_ref, scaled1_ref, p0_ref, p1_ref, q0_ref, q1_ref, lead_ref,
+    value0_ref, value1_ref, scaled0_ref, scaled1_ref, p0_ref, p1_ref, q0_ref, q1_ref, tails_ref, lead_ref,
     own_ref, next_ref, burst_ref, next_burst_ref, ends_ref, carry_ref, reach_ref, incoming_ref, logs_ref,
     a_ref, c_ref, pair_out_ref, pair_in_ref, before_ref, chips_ref, groups_ref,
     member_logs_ref, group_logs_ref, group_log_ref, chip_out_ref, group_out_ref, give_ref, take_ref,
@@ -182,15 +182,17 @@
     burst_ref[:, runs:128] = jnp.ones((8, 128 - runs), F32)
     logs_ref[...] = jnp.broadcast_to(jnp.sum(jnp.log(line), axis=1, keepdims=True), (1, 128))
 
-    pl.semaphore_wait(barrier, 2 + (MEMBERS - 1) + (groups - 1))
-    burst_copy.start()
-    for device in members:
-        remote(logs_ref, member_logs_ref.at[member], logs_sem.at[0], logs_sem.at[1], device).start()
-    for i in range(4):
-        noise(i).start()
+    def meet():
+        pl.semaphore_wait(barrier, 2 + (MEMBERS - 1) + (groups - 1))
+        burst_copy.start()
+        for device in members:
+            remote(logs_ref, member_logs_ref.at[member], logs_sem.at[0], logs_sem.at[1], device).start()
+        for i in range(4):
+            noise(i).start()
+
+    pl.when(chip >= chips // 2)(meet)
     for lane in range(4, 8):
         table(lane).start()
-
     ends_ref[0] = broadcasts(burst_ref, own_ref)
     arrived(e_ref.at[pl.ds(0, 4)], e_sem.at[0])
     lax.fori_loop(0, 4, fold_step, 0)
@@ -253,6 +255,18 @@
             a_ref[pl.ds(lane, 1), :] = here[7:8, :]
             c_ref[pl.ds(lane, 1), :] = there[7:8, :]
 
+    def tail_scan(i, tail):
+        for side in range(2):
+            lane = 2 * i + side
+            keep, keep_run, spread = rate_rows(lane)
+            there = jnp.zeros((8, 128), F32)
+            for j in range(runs):
+                at = slice(8 * j, 8 * j + 8)
+                force = weighted(tail(at, slice(128 * side, 128 * side + 128)), next_ref[1, at, :], next_ref[2, at, :], spread)
+                there = (next_ref[0, at, :] * keep) * there + force
+            there, _ = over_runs(there, ends_ref[1] * keep_run)
+            c_ref[pl.ds(lane, 1), :] = there[7:8, :]
+
     def whole(scan, i, slot):
         scan(i, slot, [None, None], 0, 1)
 
@@ -279,7 +293,6 @@
         scale(0, 0, part)
     arrived(inverse_ref, t_sem.at[3])
     def early_pair(u, carry):
-        noise(4 + u).start()
         arrived(e_ref.at[pl.ds(pl.multiple_of(4 * u + 4, 4), 4)], e_sem.at[u + 1])
 
         @pl.when(u == 0)
@@ -291,11 +304,24 @@
 
         early_step(2 * u + 1, 1, 4 * u + 6)
 
+        pl.when((u == 0) & (chip < chips // 2))(meet)
+
+        @pl.when(u < 2)
+        def _():
+            noise(4 + u).start()
+
         @pl.when(u == 0)
+        def _():
+            for slot in range(2):
+                tails_ref[slot] = ps[slot][...] + qs[slot][...]
+
+        @pl.when(u == 1)
         def _():
             burst_copy.wait()
             ends_ref[1] = broadcasts(next_burst_ref, next_ref)
-            whole(early_scan, 0, 0)
+            for k in range(2):
+                tail_scan(k, lambda at, cut: tails_ref[k, at, cut])
+            tail_scan(2, lambda at, cut: ps[0][at, cut] + qs[0][at, cut])
 
         return carry
 
@@ -306,7 +332,7 @@
         early_inverse(1, part)
         early_scan(chunks - 2, 0, states, part, 4)
     whole(early_scan, chunks - 1, 1)
-    sent_early = chunks // 2 + 3
+    sent_early = chunks // 2 + 2
 
     own_half = pl.ds(pl.multiple_of(core * 8, 8), 8)
     other_half = pl.ds(pl.multiple_of((1 - core) * 8, 8), 8)
@@ -439,11 +465,12 @@
         @pl.when(u == 0)
         def _():
             exchange_chips()
-            noise(sent_early).start()
-
-        pl.when(u == 2)(exchange_groups)
+            for i in range(sent_early, chunks):
+                noise(i).start()
+
         arrive(2 * u + 2)
         late_step(2 * u + 1, 1)
+        pl.when(u == 1)(exchange_groups)
         return carry
 
     lax.fori_loop(0, chunks // 2 - 1, late_pair, 0)
@@ -540,6 +567,7 @@
             pltpu.VMEM((length, chunk), F32),
             pltpu.VMEM((length, chunk), F32),
             pltpu.VMEM((length, chunk), F32),
+            pltpu.VMEM((2, length, chunk), F32),
             pltpu.VMEM((lanes, length, 128), F32),
             pltpu.VMEM((3, length, 128), F32),
             pltpu.VMEM((3, length, 128), F32),

time: 37.4 us -> 37.6 us (level)
  no operation moved by 1% of the time
where the time goes in v4:
time: 37.6 us; the launch traced here: 37.5 us
  Pallas kernels  37.5 us (100%)
    pallas_call x1, Pallas kernels, shards(): pl.pallas_call(functools.partial(fields, length, sections), name='fields'...  35.7 us
    pallas_call x1, Pallas kernels, shards(): pl.pallas_call(functools.partial(close, length), name='close', out_shape=...  1.72 us

profile of v4, /device:TPU:1, one launch (start us, length us, event | category | flops | bytes accessed | tf_op | source)
XLA Modules:
  0.0 37.5 jit_solution(1779627807497250524)
XLA Ops:
  0.0 35.7 %fields.1.x_ref = f32[18,392,128]{2,1,0:T(8,128)S(1)} custom-call(bf16[384,2048]{1,0:T(8,128)(2,1)} %v_hbm.1, f32[768,2048]{1,0:T(8,128)} %e_hbm.1, bf16[768,768]{1,0:T(8,128)(2,1)} %constant.4.clone.forward_hbm, bf16[384,1536]{1,0:T(8,128)(2,1)} %constant.5.clone.inverse_hbm, f32[16,128]{1,0:T(8,128)} %bitcast.3, f32[3,128]{1,0:T(4,128)} %bitcast.4), custom_call_target="tpu_custom_call" | custom-call | tf_op jit(solution)/shard_map/fields/pallas_call | solution.py:546
  35.7 1.7 %close.1 = f32[8,48,2048]{2,1,0:T(8,128)} custom-call(f32[18,392,128]{2,1,0:T(8,128)S(1)} %fields.1.x_ref), custom_call_target="tpu_custom_call" | custom-call | tf_op jit(solution)/shard_map/close/pallas_call | solution.py:617
